TPU v7x, 32 devices: a whole 2x2x4 slice. The times are simulated.
32 devices in a mesh: replica: 4 (over y, core), fsdp: 8 (over z, x).
Axes of the slice: x: 2, y: 2, z: 4, core: 2. Of those that a mesh axis runs over, the one named last changes fastest.
Arguments:
- hidden_states: bfloat16 [4, 2048, 4096], P('replica', 'fsdp'), may hold values from -6 to 6
- norm_gain: bfloat16 [4, 4096], P('replica', 'fsdp'), may hold values from 0.5 to 1.5
- key_weight: bfloat16 [4, 4096, 1024], P('replica', 'fsdp'), may hold values from -0.09375 to 0.09375
- value_weight: bfloat16 [4, 4096, 1024], P('replica', 'fsdp'), may hold values from -0.09375 to 0.09375
- deltas: float32 [4, 256, 4096], P('replica', 'fsdp'), may hold values from -6 to 6
- outer_params: float32 [256, 4096], P('fsdp', 'replica'), may hold values from -6 to 6
- momentum: float32 [256, 4096], P('fsdp', 'replica'), may hold values from -3 to 3
- local_params: bfloat16 [4, 256, 4096], P('replica', 'fsdp'), may hold values from -6 to 6
Outputs:
- keys: bfloat16 [4, 2048, 1024], P('replica', 'fsdp')
- values: bfloat16 [4, 2048, 1024], P('replica', 'fsdp')
- momentum_new: float32 [256, 4096], P('fsdp', 'replica')
- outer_new: float32 [256, 4096], P('fsdp', 'replica')
- local_new: bfloat16 [4, 256, 4096], P('replica', 'fsdp')
All inputs are finite; a program needn't handle non-finite values.
Results may differ from a plain program's by a relative error of at most 0.0085.
Values may be sent and summed in bfloat16 or wider, within the bound.
A program may use at most 128 MiB of HBM per device.

v0:
```python
import functools

import jax
import jax.numpy as jnp
import numpy as np
from jax import lax
from jax.experimental import pallas as pl
from jax.experimental.pallas import tpu as pltpu
from jax.sharding import PartitionSpec as P

HEAD = 128
MESH = pl.DeviceIdType.MESH


def rotation_tables(tokens, head_size):
    half_width = head_size // 2
    exponent = np.arange(half_width, dtype=np.float32) * np.float32(2.0 / head_size)
    frequency = np.power(np.float32(500000.0), -exponent)
    angles = np.arange(tokens, dtype=np.float32)[:, None] * frequency[None, :]
    cosine, sine = np.cos(angles), np.sin(angles)
    return (
        jnp.asarray(np.concatenate([cosine, cosine], axis=1)),
        jnp.asarray(np.concatenate([-sine, sine], axis=1)),
    )


def write_out(*refs):
    count = len(refs) // 2
    sems = refs[-1]
    copies = [
        pltpu.make_async_copy(refs[i], refs[count + i], sems.at[i]) for i in range(count)
    ]
    for copy in copies:
        copy.start()
    for copy in copies:
        copy.wait()


def stage_plan(groups):
    plan, left, bit = [], list(range(groups)), 1
    while bit < groups:
        plan.append((bit, [b for b in left if b & bit], [b for b in left if not b & bit]))
        left = plan[-1][2]
        bit *= 2
    return plan


def kernel(
    groups, replicas, width,
    hs, gain, kw, vw, cosine_in, sine_in, deltas, outer_in, momentum_in, local_in,
    keys_out, values_out, momentum_out, outer_out, local_out,
    cosine, sine, deltas_own, outer, momentum, local,
    keys, values, momentum_new, outer_new, local_new,
    hs_v, gains, a_in, a_scaled, weights, inv, partial, d_in, o_in, *rest,
):
    plan = stage_plan(groups)
    stages = len(plan)
    c_out, c_in, rest = rest[:stages], rest[stages : 2 * stages], rest[2 * stages :]
    hs_sem, g_sem, a_sem, b_sem, own_sem, c_sem, d_sem, o_sem, load_sem, store_sem = rest

    r, f = lax.axis_index("replica"), lax.axis_index("fsdp")
    x, z = lax.rem(f, 2), lax.div(f, 2)
    tokens, depth = hs.shape[0], kw.shape[0]
    quarter = 2 * depth
    per_weight = kw.shape[1] // width
    chunks = 2 * per_weight
    own_w = outer.shape[1]

    def group_at(offset):
        g, bit = z, 1
        while bit < groups:
            if offset & bit:
                g = g + bit * (1 - 2 * lax.rem(lax.div(g, bit), 2))
            bit *= 2
        return g

    def peer(offset):
        return {"fsdp": 2 * group_at(offset) + x}

    partner = {"fsdp": f + 1 - 2 * x}

    def replica_at(j):
        return lax.rem(r + j, replicas)

    barrier = pltpu.get_barrier_semaphore()
    pl.semaphore_signal(barrier, inc=1, device_id=partner, device_id_type=MESH)
    for b in range(1, groups):
        pl.semaphore_signal(barrier, inc=1, device_id=peer(b), device_id_type=MESH)
    for j in range(1, replicas):
        pl.semaphore_signal(
            barrier, inc=1, device_id={"replica": replica_at(j)}, device_id_type=MESH
        )

    def remote(src, dst, sems, index, target):
        return pltpu.make_async_remote_copy(
            src_ref=src, dst_ref=dst, send_sem=sems.at[(0,) + index],
            recv_sem=sems.at[(1,) + index], device_id=target, device_id_type=MESH,
        )

    mine = pl.ds(pl.multiple_of(r * own_w, own_w), own_w)
    hs_copy = pltpu.make_async_copy(hs, hs_v, hs_sem)
    hs_copy.start()
    loads = [
        pltpu.make_async_copy(source, target, load_sem.at[i])
        for i, (source, target) in enumerate(
            (
                (deltas.at[:, mine], deltas_own),
                (outer_in, outer),
                (momentum_in, momentum),
                (local_in, local),
                (cosine_in, cosine),
                (sine_in, sine),
            )
        )
    ]
    rows = pl.ds(pl.multiple_of(x * depth, depth), depth)
    own_copies = []
    for c in range(chunks):
        source = (kw if c < per_weight else vw).at[:, pl.ds((c % per_weight) * width, width)]
        own_copies.append(pltpu.make_async_copy(source, weights.at[c, rows], own_sem.at[c]))
        own_copies[-1].start()

    pl.semaphore_wait(barrier, groups + replicas - 1)

    gain_copy = remote(gain, gains.at[x], g_sem, (), partner)
    gain_copy.start()
    a_copies = {}

    def send_tokens(offsets):
        for b in offsets:
            columns = pl.ds(pl.multiple_of(group_at(b) * quarter, quarter), quarter)
            a_copies[b] = remote(hs.at[:, columns], a_in.at[b - 1], a_sem, (b - 1,), peer(b))
            a_copies[b].start()

    send_tokens(plan[0][1][::-1] + [b for b in plan[0][2] if b])
    b_copies = []
    for c in range(chunks):
        source = (kw if c < per_weight else vw).at[:, pl.ds((c % per_weight) * width, width)]
        b_copies.append(remote(source, weights.at[c, rows], b_sem, (c,), partner))
        b_copies[-1].start()
    d_copies = []
    for j in range(1, replicas):
        columns = pl.ds(pl.multiple_of(replica_at(j) * own_w, own_w), own_w)
        d_copies.append(
            remote(
                deltas.at[:, columns], d_in.at[j - 1], d_sem, (j - 1,), {"replica": replica_at(j)}
            )
        )
        d_copies[-1].start()

    for copy in loads:
        copy.start()

    def store(i, source, target):
        copy = pltpu.make_async_copy(source, target, store_sem.at[i])
        copy.start()
        return copy

    def result_copy(source, target, c, sem):
        at = pl.ds(pl.multiple_of(c * width, width), width)
        return pltpu.make_async_copy(source.at[:, at], target.at[:, at], store_sem.at[sem])

    def c_copy(stage, c):
        return remote(
            c_out[stage].at[c], c_in[stage].at[c], c_sem, (stage, c), peer(plan[stage][0])
        )

    def b_wait(c):
        pltpu.make_async_copy(
            kw.at[:, pl.ds(0, width)], weights.at[c, rows], own_sem.at[c]
        ).wait()
        remote(
            kw.at[:, pl.ds(0, width)], weights.at[c, rows], b_sem, (c,), partner
        ).wait_recv()

    hs_copy.wait()
    total = jnp.zeros((tokens, 1), jnp.float32)
    features = hs.shape[1]
    for k in range(groups):
        part = hs_v[:, k * quarter : (k + 1) * quarter].astype(jnp.float32)
        total += jnp.sum(part * part, axis=1, keepdims=True)
    inv[...] = jnp.broadcast_to(lax.rsqrt(total / features + 1e-05), inv.shape)

    gains[x] = gain[...]
    gain_copy.wait()
    gain_row = jnp.concatenate([gains[0], gains[1]], axis=1).astype(jnp.float32)

    def scale(b, block):
        a_scaled[b] = (block.astype(jnp.float32) * gain_row).astype(jnp.bfloat16)

    scale(0, hs_v[:, pl.ds(pl.multiple_of(z * quarter, quarter), quarter)])
    for b in plan[0][1]:
        a_copies[b].wait_recv()
        scale(b, a_in[b - 1])

    def product(b, c):
        return jnp.dot(a_scaled[b], weights[c], preferred_element_type=jnp.float32)

    def first_products(c):
        b_wait(c)
        for i, b in enumerate(plan[0][1]):
            c_out[0][c, i] = product(b, c).astype(jnp.bfloat16)
        c_copy(0, c).start()

    pl.loop(0, chunks)(first_products)

    for copy in loads:
        copy.wait()
    avg = deltas_own[...]
    for j in range(1, replicas):
        d_copies[j - 1].wait_recv()
        avg += d_in[j - 1]
    avg = avg / replicas
    moved = 0.9 * momentum[...] + avg
    momentum_new[...] = moved
    outer_new[...] = outer[...] - 0.7 * (avg + 0.9 * moved)
    stores = [store(0, momentum_new, momentum_out), store(1, outer_new, outer_out)]

    for b in plan[0][2]:
        if b:
            a_copies[b].wait_recv()
            scale(b, a_in[b - 1])

    o_copies = []
    for j in range(1, replicas):
        o_copies.append(
            remote(outer_new, o_in.at[j - 1], o_sem, (j - 1,), {"replica": replica_at(j)})
        )
        o_copies[-1].start()

    for stage in range(stages):
        bit, sent, kept = plan[stage]
        last = stage == stages - 1
        upcoming = [] if last else plan[stage + 1][1]

        def summed(b, c):
            before = product(b, c) if stage == 0 else partial[b, c]
            return before + c_in[stage][c, sent.index(b + bit)].astype(jnp.float32)

        if not last:

            @pl.loop(0, chunks)
            def _(c):
                c_copy(stage, c).wait_recv()
                for b in kept:
                    value = summed(b, c)
                    if b in upcoming:
                        c_out[stage + 1][c, upcoming.index(b)] = value.astype(jnp.bfloat16)
                    else:
                        partial[b, c] = value
                c_copy(stage + 1, c).start()

        if stage == 0:
            half = jnp.float32(0.5)
            local_new[:, mine] = (
                half * local[:, mine].astype(jnp.float32) + half * outer_new[...]
            ).astype(jnp.bfloat16)
            for j in range(1, replicas):
                o_copies[j - 1].wait_recv()
                theirs = pl.ds(
                    pl.multiple_of(lax.rem(r + replicas - j, replicas) * own_w, own_w), own_w
                )
                local_new[:, theirs] = (
                    half * local[:, theirs].astype(jnp.float32) + half * o_in[j - 1]
                ).astype(jnp.bfloat16)
            stores.append(store(2, local_new, local_out))

        if last:

            @pl.loop(0, per_weight)
            def _(c):
                c_copy(stage, c).wait_recv()
                value = summed(0, c) * inv[:, 0:1]
                for h in range(width // HEAD):
                    head = value[:, h * HEAD : (h + 1) * HEAD]
                    turned = head * cosine[...] + pltpu.roll(head, HEAD // 2, 1) * sine[...]
                    at = pl.ds(pl.multiple_of(c * width + h * HEAD, HEAD), HEAD)
                    keys[:, at] = turned.astype(jnp.bfloat16)
                result_copy(keys, keys_out, c, 3 + c).start()

            @pl.loop(0, per_weight)
            def _(c):
                c_copy(stage, c + per_weight).wait_recv()
                value = summed(0, c + per_weight) * inv[:, 0:1]
                at = pl.ds(pl.multiple_of(c * width, width), width)
                values[:, at] = value.astype(jnp.bfloat16)
                result_copy(values, values_out, c, 3 + per_weight + c).start()

    for copy in stores:
        copy.wait()

    @pl.loop(0, per_weight)
    def _(c):
        result_copy(keys, keys_out, c, 3 + c).wait()
        result_copy(values, values_out, c, 3 + per_weight + c).wait()

    for copy in list(a_copies.values()) + b_copies + d_copies + o_copies:
        copy.wait_send()
    for stage in range(stages):

        @pl.loop(0, chunks)
        def _(c):
            c_copy(stage, c).wait_send()


def per_device(
    groups, replicas,
    hidden_states, norm_gain, key_weight, value_weight, deltas, outer_params, momentum, local_params,
):
    hs, kw, vw = hidden_states[0], key_weight[0], value_weight[0]
    tokens, features = hs.shape
    depth, kv = kw.shape
    width = 2 * HEAD
    chunks = 2 * kv // width
    cosine, sine = rotation_tables(tokens, HEAD)
    plan = stage_plan(groups)
    blocks = [pltpu.VMEM((chunks, len(p[1]), tokens, width), jnp.bfloat16) for p in plan]
    own = outer_params.shape
    vmem = pl.BlockSpec(memory_space=pltpu.VMEM)
    hbm = pl.BlockSpec(memory_space=pl.ANY)
    dma = pltpu.SemaphoreType.DMA
    results = pl.pallas_call(
        functools.partial(kernel, groups, replicas, width),
        out_shape=(
            jax.ShapeDtypeStruct((tokens, kv), jnp.bfloat16),
            jax.ShapeDtypeStruct((tokens, kv), jnp.bfloat16),
            jax.ShapeDtypeStruct(own, jnp.float32),
            jax.ShapeDtypeStruct(own, jnp.float32),
            jax.ShapeDtypeStruct(local_params.shape[1:], jnp.bfloat16),
        ),
        in_specs=[hbm, vmem] + [hbm] * 8,
        out_specs=[hbm] * 5,
        scratch_shapes=[
            pltpu.VMEM(cosine.shape, jnp.float32),
            pltpu.VMEM(sine.shape, jnp.float32),
            pltpu.VMEM(own, jnp.float32),
            pltpu.VMEM(own, jnp.float32),
            pltpu.VMEM(own, jnp.float32),
            pltpu.VMEM(local_params.shape[1:], jnp.bfloat16),
            pltpu.VMEM((tokens, kv), jnp.bfloat16),
            pltpu.VMEM((tokens, kv), jnp.bfloat16),
            pltpu.VMEM(own, jnp.float32),
            pltpu.VMEM(own, jnp.float32),
            pltpu.VMEM(local_params.shape[1:], jnp.bfloat16),
            pltpu.VMEM((tokens, features), jnp.bfloat16),
            pltpu.VMEM((2, 1, depth), jnp.bfloat16),
            pltpu.VMEM((groups - 1, tokens, 2 * depth), jnp.bfloat16),
            pltpu.VMEM((groups, tokens, 2 * depth), jnp.bfloat16),
            pltpu.VMEM((chunks, 2 * depth, width), jnp.bfloat16),
            pltpu.VMEM((tokens, HEAD), jnp.float32),
            pltpu.VMEM((max(p + 1 for p in plan[0][2] if not p & 2), chunks, tokens, width), jnp.float32),
            pltpu.VMEM((replicas - 1,) + own, jnp.float32),
            pltpu.VMEM((replicas - 1,) + own, jnp.float32),
            *blocks,
            *blocks,
            dma,
            dma((2,)),
            dma((2, groups - 1)),
            dma((2, chunks)),
            dma((chunks,)),
            dma((2, len(plan), chunks)),
            dma((2, replicas - 1)),
            dma((2, replicas - 1)),
            dma((6,)),
            dma((3 + chunks,)),
        ],
        compiler_params=pltpu.CompilerParams(
            collective_id=0, has_side_effects=True, vmem_limit_bytes=60 * 1024 * 1024
        ),
    )(
        hs, norm_gain, kw, vw, cosine, sine,
        deltas[0], outer_params, momentum, local_params[0],
    )
    keys, values, momentum_new, outer_new, local_new = pl.pallas_call(
        write_out,
        out_shape=tuple(jax.ShapeDtypeStruct(a.shape, a.dtype) for a in results),
        in_specs=[vmem] * 5,
        out_specs=[hbm] * 5,
        scratch_shapes=[dma((5,))],
        compiler_params=pltpu.CompilerParams(vmem_limit_bytes=60 * 1024 * 1024),
    )(*results)
    return keys[None], values[None], momentum_new, outer_new, local_new[None]


def solution(mesh):
    in_specs = (
        P("replica", "fsdp", None),
        P("replica", "fsdp"),
        P("replica", "fsdp", None),
        P("replica", "fsdp", None),
        P("replica", "fsdp", None),
        P("fsdp", "replica"),
        P("fsdp", "replica"),
        P("replica", "fsdp", None),
    )
    out_specs = (
        P("replica", "fsdp", None),
        P("replica", "fsdp", None),
        P("fsdp", "replica"),
        P("fsdp", "replica"),
        P("replica", "fsdp", None),
    )
    groups, replicas = mesh.shape["fsdp"] // 2, mesh.shape["replica"]
    return jax.shard_map(
        functools.partial(per_device, groups, replicas),
        mesh=mesh, in_specs=in_specs, out_specs=out_specs, check_vma=False,
    )
```

profile of v0, /device:TPU:0, one launch (start us, length us, event | category | flops | bytes accessed | tf_op | source)
XLA Modules:
  0.0 116.0 jit_solution(15038454619035232749)
XLA Ops:
  0.6 112.9 %shard_map.137 = (bf16[256,1024]{1,0:T(8,128)(2,1)}, bf16[256,1024]{1,0:T(8,128)(2,1)}, f32[32,1024]{1,0:T(8,128)}, f32[32,1024]{1,0:T(8,128)}, bf16[32,4096]{1,0:T(8,128)(2,1)}) custom-call(bf16[256,4096]{1,0:T(8,128)(2,1)} %bitcast.8, bf16[1,512]{1,0:T(2,128)(2,1)} %gain.1, bf16[512,1024]{1,0:T(8,128)(2,1)} %bitcast.9, bf16[512,1024]{1,0:T(8,128)(2,1)} %bitcast.10, ...), custom_call_target="tpu_custom_call" | custom-call | tf_op jit(solution)/shard_map/pallas_call | solution.py:322
  113.5 2.5 %shard_map.138 = (bf16[256,1024]{1,0:T(8,128)(2,1)}, bf16[256,1024]{1,0:T(8,128)(2,1)}, f32[32,1024]{1,0:T(8,128)}, f32[32,1024]{1,0:T(8,128)}, bf16[32,4096]{1,0:T(8,128)(2,1)}) custom-call(bf16[256,1024]{1,0:T(8,128)(2,1)} %get-tuple-element.15.refs_0_, bf16[256,1024]{1,0:T(8,128)(2,1)} %get-tuple-element.16.refs_1_, ...), custom_call_target="tpu_custom_call" | custom-call | tf_op jit(solution)/shard_map/pallas_call | solution.py:374
where the time goes:
time: 117 us; the launch traced here: 116 us
  Pallas kernels  115 us (98%)
    pallas_call x1, Pallas kernels, per_device(): pl.pallas_call(functools.partial(kernel, groups, replicas, width), out_sh...  113 us
    pallas_call x1, Pallas kernels, per_device(): pl.pallas_call(write_out, out_shape=tuple((jax.ShapeDtypeStruct(a.shape,...  2.52 us

commit v1 on v0

v1 whole, which is shorter than its diff:
```python
import functools

import jax
import jax.numpy as jnp
import numpy as np
from jax import lax
from jax.experimental import pallas as pl
from jax.experimental.pallas import tpu as pltpu
from jax.sharding import PartitionSpec as P

HEAD = 128
MESH = pl.DeviceIdType.MESH


def rotation_tables(tokens, head_size):
    half_width = head_size // 2
    exponent = np.arange(half_width, dtype=np.float32) * np.float32(2.0 / head_size)
    frequency = np.power(np.float32(500000.0), -exponent)
    angles = np.arange(tokens, dtype=np.float32)[:, None] * frequency[None, :]
    cosine, sine = np.cos(angles), np.sin(angles)
    return (
        jnp.asarray(np.concatenate([cosine, cosine], axis=1)),
        jnp.asarray(np.concatenate([-sine, sine], axis=1)),
    )


def write_out(*refs):
    count = len(refs) // 2
    sems = refs[-1]
    copies = [
        pltpu.make_async_copy(refs[i], refs[count + i], sems.at[i]) for i in range(count)
    ]
    for copy in copies:
        copy.start()
    for copy in copies:
        copy.wait()


def kernel(
    groups, replicas, width,
    hs, gain, kw, vw, cosine_in, sine_in, deltas, outer_in, momentum_in, local_in,
    keys_out, values_out, momentum_out, outer_out, local_out,
    cosine, sine, deltas_own, outer, momentum, local,
    keys, values, momentum_new, outer_new, local_new,
    hs_v, gains, a_in, a_scaled, a_own, weights, inv, acc, c_out, c_in, d_in, o_in,
    hs_sem, g_sem, a_sem, own_sem, w_recv, x_send, z_send, f_send, e_send,
    c_send, c_recv, d_sem, o_sem, load_sem, store_sem,
):
    h = groups // 2
    r, f = lax.axis_index("replica"), lax.axis_index("fsdp")
    x, g = lax.rem(f, 2), lax.div(f, 2)
    half = lax.div(g, h)
    local_g = lax.rem(g, h)
    d = (h - 1 - local_g) * (1 - half) + local_g * half
    tokens, depth = hs.shape[0], kw.shape[0]
    half_depth = 2 * h * depth
    per_weight = kw.shape[1] // width
    chunks = 2 * per_weight
    first = chunks // 2
    split = chunks - chunks // 4
    early = chunks // 4
    own_w = outer.shape[1]
    features = hs.shape[1]

    def place(dist):
        return (h - 1 - dist) * (1 - half) + dist * half

    def slot(dist, side):
        return 2 * place(dist) + side

    def device(dist, side):
        return {"fsdp": 2 * (half * h + place(dist)) + side}

    def other_half(dist):
        return {"fsdp": 2 * ((1 - half) * (h + dist) + half * (h - 1 - dist)) + x}

    partner = device(d, 1 - x)
    outer_peers = [(0, True)] + [(1 + lax.rem(d - 1 + j, h - 1), False) for j in range(1, h - 1)]
    inner_peers = [(j, False) for j in range(1, h)]
    is_inner = d == 0

    def replica_at(j):
        return lax.rem(r + j, replicas)

    def mates():
        me = 2 * local_g + x
        return [
            {"fsdp": half * 2 * h + lax.rem(me + j, 2 * h)} for j in range(1, 2 * h)
        ]

    barrier = pltpu.get_barrier_semaphore()

    def greet(target):
        pl.semaphore_signal(barrier, inc=1, device_id=target, device_id_type=MESH)

    for target in mates():
        greet(target)
    greet(other_half(0))
    for j in range(1, replicas):
        greet({"replica": replica_at(j)})

    @pl.when(is_inner)
    def _():
        for i in range(h):
            greet(other_half(i))

    def remote(src, dst, send, recv, target):
        return pltpu.make_async_remote_copy(
            src_ref=src, dst_ref=dst, send_sem=send, recv_sem=recv,
            device_id=target, device_id_type=MESH,
        )

    mine = pl.ds(pl.multiple_of(r * own_w, own_w), own_w)
    hs_copy = pltpu.make_async_copy(hs, hs_v, hs_sem)
    hs_copy.start()
    my_slot = slot(d, x)
    partner_slot = slot(d, 1 - x)

    def rows(q):
        return pl.ds(pl.multiple_of(q * depth, depth), depth)

    def source(c):
        return (kw if c < per_weight else vw).at[:, pl.ds((c % per_weight) * width, width)]

    own_copies = []
    for c in range(chunks):
        own_copies.append(
            pltpu.make_async_copy(source(c), weights.at[c, rows(my_slot)], own_sem.at[c])
        )
        own_copies[-1].start()
    loads = [
        pltpu.make_async_copy(src, dst, load_sem.at[i])
        for i, (src, dst) in enumerate(
            (
                (deltas.at[:, mine], deltas_own),
                (outer_in, outer),
                (momentum_in, momentum),
                (local_in, local),
                (cosine_in, cosine),
                (sine_in, sine),
            )
        )
    ]

    pl.semaphore_wait(
        barrier, (2 * h - 1) + 1 + (replicas - 1) + jnp.where(is_inner, h, 0)
    )

    def x_copy(c):
        return remote(
            source(c), weights.at[c, rows(my_slot)], x_send.at[c], w_recv.at[c, my_slot], partner
        )

    def z_copy(c, j, dist):
        return remote(
            source(c), weights.at[c, rows(my_slot)], z_send.at[j, c], w_recv.at[c, my_slot],
            device(dist, x),
        )

    def f_copy(c, j, dist):
        q = slot(dist, x)
        return remote(
            weights.at[c, rows(q)], weights.at[c, rows(q)], f_send.at[j, c], w_recv.at[c, q],
            partner,
        )

    def e_copy(c, j, dist):
        return remote(
            weights.at[c, rows(partner_slot)], weights.at[c, rows(partner_slot)],
            e_send.at[j, c], w_recv.at[c, partner_slot], device(dist, x),
        )

    def arrived(c, q):
        remote(
            kw.at[:, pl.ds(0, width)], weights.at[c, rows(q)], x_send.at[0], w_recv.at[c, q],
            partner,
        ).wait_recv()

    away = pl.ds(pl.multiple_of((1 - half) * half_depth, half_depth), half_depth)
    a_copy = remote(hs.at[:, away], a_in.at[d], a_sem.at[0], a_sem.at[1 + d], other_half(0))

    @pl.when(is_inner)
    def _():
        for c in range(2):
            x_copy(c).start()
        a_copy.start()
        for c in range(chunks):
            for j, (dist, _) in enumerate(inner_peers):
                z_copy(c, j, dist).start()

    @pl.when(jnp.logical_not(is_inner))
    def _():
        for c in range(chunks):
            if c == first:
                a_copy.start()
            for j, (dist, _) in enumerate(outer_peers):
                z_copy(c, j, dist).start()
        for c in list(range(split, chunks)) + list(range(early)):
            x_copy(c).start()

    g_copies = []
    for j, target in enumerate(mates()):
        g_copies.append(
            remote(gain, gains.at[my_slot], g_sem.at[j], g_sem.at[2 * h - 1 + my_slot], target)
        )
        g_copies[-1].start()
    d_copies = []
    for j in range(1, replicas):
        columns = pl.ds(pl.multiple_of(replica_at(j) * own_w, own_w), own_w)
        d_copies.append(
            remote(
                deltas.at[:, columns], d_in.at[j - 1], d_sem.at[0, j - 1], d_sem.at[1, j - 1],
                {"replica": replica_at(j)},
            )
        )
        d_copies[-1].start()
    for copy in loads:
        copy.start()

    hs_copy.wait()
    total = jnp.zeros((tokens, 1), jnp.float32)
    part_w = 2 * depth
    for k in range(features // part_w):
        part = hs_v[:, k * part_w : (k + 1) * part_w].astype(jnp.float32)
        total += jnp.sum(part * part, axis=1, keepdims=True)
    inv[...] = jnp.broadcast_to(lax.rsqrt(total / features + 1e-05), inv.shape)

    gains[my_slot] = gain[...]
    for j in range(1, 2 * h):
        q = lax.rem(my_slot + j, 2 * h)
        remote(gain, gains.at[q], g_sem.at[0], g_sem.at[2 * h - 1 + q], partner).wait_recv()

    def scale(target, origin, base):
        for q in range(2 * h):
            at = pl.ds(base + q * depth, depth)
            target[:, q * depth : (q + 1) * depth] = (
                origin[:, at].astype(jnp.float32) * gains[q].astype(jnp.float32)
            ).astype(jnp.bfloat16)

    @pl.when(half == 0)
    def _():
        scale(a_own, hs_v, 0)

    @pl.when(half == 1)
    def _():
        scale(a_own, hs_v, half_depth)

    def own_product(c):
        acc[c] = jnp.dot(a_own[...], weights[c], preferred_element_type=jnp.float32)

    def back_copy(i, c):
        return remote(c_out.at[i, c], c_in.at[c], c_send.at[i, c], c_recv.at[c], other_half(i))

    def away_product(i, c):
        c_out[i, c] = jnp.dot(
            a_scaled[i], weights[c], preferred_element_type=jnp.float32
        ).astype(jnp.bfloat16)
        back_copy(i, c).start()

    def own_wait(c):
        pltpu.make_async_copy(
            kw.at[:, pl.ds(0, width)], weights.at[c, rows(my_slot)], own_sem.at[c]
        ).wait()

    def outer_step():
        for copy in loads:
            copy.wait()
        avg = deltas_own[...]
        for j in range(1, replicas):
            d_copies[j - 1].wait_recv()
            avg += d_in[j - 1]
        avg = avg / replicas
        moved = 0.9 * momentum[...] + avg
        momentum_new[...] = moved
        outer_new[...] = outer[...] - 0.7 * (avg + 0.9 * moved)
        store(0, momentum_new, momentum_out).start()
        store(1, outer_new, outer_out).start()
        for j in range(1, replicas):
            o_copy(j).start()

    def merge_step():
        part = jnp.float32(0.5)
        local_new[:, mine] = (
            part * local[:, mine].astype(jnp.float32) + part * outer_new[...]
        ).astype(jnp.bfloat16)
        for j in range(1, replicas):
            o_copy(j).wait_recv()
            theirs = pl.ds(
                pl.multiple_of(lax.rem(r + replicas - j, replicas) * own_w, own_w), own_w
            )
            local_new[:, theirs] = (
                part * local[:, theirs].astype(jnp.float32) + part * o_in[j - 1]
            ).astype(jnp.bfloat16)
        store(2, local_new, local_out).start()

    def o_copy(j):
        return remote(
            outer_new, o_in.at[j - 1], o_sem.at[0, j - 1], o_sem.at[1, j - 1],
            {"replica": replica_at(j)},
        )

    def store(i, src, dst):
        return pltpu.make_async_copy(src, dst, store_sem.at[i])

    def result_copy(src, dst, c, sem):
        at = pl.ds(pl.multiple_of(c * width, width), width)
        return pltpu.make_async_copy(src.at[:, at], dst.at[:, at], store_sem.at[sem])

    @pl.when(is_inner)
    def _():
        def pass_on(c):
            for j, (dist, _) in enumerate(inner_peers):
                arrived(c, slot(dist, x))
                if c < split:
                    f_copy(c, j, dist).start()

        for c in range(first):
            pass_on(c)
            if c + 2 < first:
                x_copy(c + 2).start()
            if c < early:
                arrived(c, partner_slot)
                for j, (dist, _) in enumerate(inner_peers):
                    e_copy(c, j, dist).start()
            if c == 0:
                outer_step()
            if c == 1:
                merge_step()
        for c in range(first, split):
            x_copy(c).start()

        def rest(c, known):
            own_wait(c)
            if not known:
                arrived(c, partner_slot)
            for dist, _ in inner_peers:
                arrived(c, slot(dist, 1 - x))

        remote(hs.at[:, away], a_in.at[0], a_sem.at[0], a_sem.at[1], partner).wait_recv()
        for q in range(2 * h):
            at = slice(q * depth, (q + 1) * depth)
            a_scaled[0, :, at] = (
                a_in[0, :, at].astype(jnp.float32) * gains[q].astype(jnp.float32)
            ).astype(jnp.bfloat16)

        @pl.loop(0, early)
        def _(c):
            rest(c, True)
            away_product(0, c)
            own_product(c)

        @pl.loop(early, first)
        def _(c):
            rest(c, False)
            away_product(0, c)
            own_product(c)

        for i in range(1, h):
            remote(
                hs.at[:, away], a_in.at[i], a_sem.at[0], a_sem.at[1 + i], partner
            ).wait_recv()
            for q in range(2 * h):
                at = slice(q * depth, (q + 1) * depth)
                a_scaled[i, :, at] = (
                    a_in[i, :, at].astype(jnp.float32) * gains[q].astype(jnp.float32)
                ).astype(jnp.bfloat16)

            @pl.loop(0, first)
            def _(c):
                away_product(i, c)

        pass_on(first)
        for c in range(first, chunks):
            if c + 1 < chunks:
                pass_on(c + 1)
            if c + 1 == split - 1:
                for k in range(split, chunks):
                    x_copy(k).start()
            rest(c, False)
            for i in range(h):
                away_product(i, c)
            own_product(c)

    @pl.when(jnp.logical_not(is_inner))
    def _():
        for c in range(chunks):
            for j, (dist, _) in enumerate(outer_peers):
                arrived(c, slot(dist, x))
                if c >= early:
                    f_copy(c, j, dist).start()
            if early <= c < split:
                x_copy(c).start()
            if c == 1:
                for k in range(split, chunks):
                    arrived(k, partner_slot)
                    for j, (dist, inner) in enumerate(outer_peers):
                        if inner:
                            e_copy(k, j, dist).start()
                outer_step()
            if c == 2:
                for k in range(early):
                    arrived(k, partner_slot)
                    for j, (dist, inner) in enumerate(outer_peers):
                        if not inner:
                            e_copy(k, j, dist).start()
                merge_step()

        def finish(c, known):
            own_wait(c)
            if not known:
                arrived(c, partner_slot)
            for dist, _ in outer_peers:
                arrived(c, slot(dist, 1 - x))
            own_product(c)

        @pl.loop(early, split)
        def _(c):
            finish(c, False)

        @pl.loop(0, early)
        def _(c):
            finish(c, True)

        @pl.loop(split, chunks)
        def _(c):
            finish(c, True)

    def summed(c):
        back_copy(0, c).wait_recv()
        return (acc[c] + c_in[c].astype(jnp.float32)) * inv[:, 0:1]

    @pl.loop(0, per_weight)
    def _(c):
        value = summed(c)
        for k in range(width // HEAD):
            head = value[:, k * HEAD : (k + 1) * HEAD]
            turned = head * cosine[...] + pltpu.roll(head, HEAD // 2, 1) * sine[...]
            at = pl.ds(pl.multiple_of(c * width + k * HEAD, HEAD), HEAD)
            keys[:, at] = turned.astype(jnp.bfloat16)
        result_copy(keys, keys_out, c, 3 + c).start()

    @pl.loop(0, per_weight)
    def _(c):
        at = pl.ds(pl.multiple_of(c * width, width), width)
        values[:, at] = summed(c + per_weight).astype(jnp.bfloat16)
        result_copy(values, values_out, c, 3 + per_weight + c).start()

    a_copy.wait_send()
    for copy in g_copies + d_copies:
        copy.wait_send()
    for j in range(1, replicas):
        o_copy(j).wait_send()

    @pl.loop(0, chunks)
    def _(c):
        remote(
            kw.at[:, pl.ds(0, width)], weights.at[c, rows(my_slot)], x_send.at[c],
            w_recv.at[c, my_slot], partner,
        ).wait_send()
        for j in range(h - 1):
            remote(
                kw.at[:, pl.ds(0, width)], weights.at[c, rows(my_slot)], z_send.at[j, c],
                w_recv.at[c, my_slot], partner,
            ).wait_send()

    @pl.when(is_inner)
    def _():
        @pl.loop(0, chunks)
        def _(c):
            for i in range(h):
                back_copy(i, c).wait_send()

        for j, (dist, _) in enumerate(inner_peers):
            for c in range(split):
                f_copy(c, j, dist).wait_send()
            for c in range(early):
                e_copy(c, j, dist).wait_send()

    @pl.when(jnp.logical_not(is_inner))
    def _():
        for j, (dist, inner) in enumerate(outer_peers):
            for c in range(early, chunks):
                f_copy(c, j, dist).wait_send()
            for c in range(split, chunks) if inner else range(early):
                e_copy(c, j, dist).wait_send()

    store(0, momentum_new, momentum_out).wait()
    store(1, outer_new, outer_out).wait()
    store(2, local_new, local_out).wait()

    @pl.loop(0, per_weight)
    def _(c):
        result_copy(keys, keys_out, c, 3 + c).wait()
        result_copy(values, values_out, c, 3 + per_weight + c).wait()


def per_device(
    groups, replicas,
    hidden_states, norm_gain, key_weight, value_weight, deltas, outer_params, momentum, local_params,
):
    hs, kw, vw = hidden_states[0], key_weight[0], value_weight[0]
    tokens, features = hs.shape
    depth, kv = kw.shape
    width = 2 * HEAD
    chunks = 2 * kv // width
    h = groups // 2
    half_depth = groups * depth
    cosine, sine = rotation_tables(tokens, HEAD)
    own = outer_params.shape
    vmem = pl.BlockSpec(memory_space=pltpu.VMEM)
    hbm = pl.BlockSpec(memory_space=pl.ANY)
    dma = pltpu.SemaphoreType.DMA
    bf16, f32 = jnp.bfloat16, jnp.float32
    results = pl.pallas_call(
        functools.partial(kernel, groups, replicas, width),
        out_shape=(
            jax.ShapeDtypeStruct((tokens, kv), bf16),
            jax.ShapeDtypeStruct((tokens, kv), bf16),
            jax.ShapeDtypeStruct(own, f32),
            jax.ShapeDtypeStruct(own, f32),
            jax.ShapeDtypeStruct(local_params.shape[1:], bf16),
        ),
        in_specs=[hbm, vmem] + [hbm] * 8,
        out_specs=[hbm] * 5,
        scratch_shapes=[
            pltpu.VMEM(cosine.shape, f32),
            pltpu.VMEM(sine.shape, f32),
            pltpu.VMEM(own, f32),
            pltpu.VMEM(own, f32),
            pltpu.VMEM(own, f32),
            pltpu.VMEM(local_params.shape[1:], bf16),
            pltpu.VMEM((tokens, kv), bf16),
            pltpu.VMEM((tokens, kv), bf16),
            pltpu.VMEM(own, f32),
            pltpu.VMEM(own, f32),
            pltpu.VMEM(local_params.shape[1:], bf16),
            pltpu.VMEM((tokens, features), bf16),
            pltpu.VMEM((2 * h, 1, depth), bf16),
            pltpu.VMEM((h, tokens, half_depth), bf16),
            pltpu.VMEM((h, tokens, half_depth), bf16),
            pltpu.VMEM((tokens, half_depth), bf16),
            pltpu.VMEM((chunks, half_depth, width), bf16),
            pltpu.VMEM((tokens, HEAD), f32),
            pltpu.VMEM((chunks, tokens, width), f32),
            pltpu.VMEM((h, chunks, tokens, width), bf16),
            pltpu.VMEM((chunks, tokens, width), bf16),
            pltpu.VMEM((replicas - 1,) + own, f32),
            pltpu.VMEM((replicas - 1,) + own, f32),
            dma,
            dma((4 * h - 1,)),
            dma((1 + h,)),
            dma((chunks,)),
            dma((chunks, 2 * h)),
            dma((chunks,)),
            dma((h - 1, chunks)),
            dma((h - 1, chunks)),
            dma((h - 1, chunks)),
            dma((h, chunks)),
            dma((chunks,)),
            dma((2, replicas - 1)),
            dma((2, replicas - 1)),
            dma((6,)),
            dma((3 + chunks,)),
        ],
        compiler_params=pltpu.CompilerParams(
            collective_id=0, has_side_effects=True, vmem_limit_bytes=60 * 1024 * 1024
        ),
    )(
        hs, norm_gain, kw, vw, cosine, sine,
        deltas[0], outer_params, momentum, local_params[0],
    )
    keys, values, momentum_new, outer_new, local_new = pl.pallas_call(
        write_out,
        out_shape=tuple(jax.ShapeDtypeStruct(a.shape, a.dtype) for a in results),
        in_specs=[vmem] * 5,
        out_specs=[hbm] * 5,
        scratch_shapes=[dma((5,))],
        compiler_params=pltpu.CompilerParams(vmem_limit_bytes=60 * 1024 * 1024),
    )(*results)
    return keys[None], values[None], momentum_new, outer_new, local_new[None]


def solution(mesh):
    in_specs = (
        P("replica", "fsdp", None),
        P("replica", "fsdp"),
        P("replica", "fsdp", None),
        P("replica", "fsdp", None),
        P("replica", "fsdp", None),
        P("fsdp", "replica"),
        P("fsdp", "replica"),
        P("replica", "fsdp", None),
    )
    out_specs = (
        P("replica", "fsdp", None),
        P("replica", "fsdp", None),
        P("fsdp", "replica"),
        P("fsdp", "replica"),
        P("replica", "fsdp", None),
    )
    groups, replicas = mesh.shape["fsdp"] // 2, mesh.shape["replica"]
    return jax.shard_map(
        functools.partial(per_device, groups, replicas),
        mesh=mesh, in_specs=in_specs, out_specs=out_specs, check_vma=False,
    )
```

time: 117 us -> 158 us (1.35)
  Pallas kernels: 115 us -> 157 us
    pallas_call x1, Pallas kernels: 113 us -> 155 us  [per_device(): pl.pallas_call(functools.partial(kernel, groups, replicas, width), out_sh...]
where the time goes in v1:
time: 158 us
  Pallas kernels  157 us (99%)
    pallas_call x1, Pallas kernels, per_device(): pl.pallas_call(functools.partial(kernel, groups, replicas, width), out_sh...  155 us

profile of v1, /device:TPU:0, one launch (start us, length us, event | category | flops | bytes accessed | tf_op | source)
XLA Modules:
  0.0 157.9 jit_solution(6029721058214549925)
XLA Ops:
  0.6 154.8 %shard_map.137 = (bf16[256,1024]{1,0:T(8,128)(2,1)}, bf16[256,1024]{1,0:T(8,128)(2,1)}, f32[32,1024]{1,0:T(8,128)}, f32[32,1024]{1,0:T(8,128)}, bf16[32,4096]{1,0:T(8,128)(2,1)}) custom-call(bf16[256,4096]{1,0:T(8,128)(2,1)} %bitcast.8, bf16[1,512]{1,0:T(2,128)(2,1)} %gain.1, bf16[512,1024]{1,0:T(8,128)(2,1)} %bitcast.9, bf16[512,1024]{1,0:T(8,128)(2,1)} %bitcast.10, ...), custom_call_target="tpu_custom_call" | custom-call | tf_op jit(solution)/shard_map/pallas_call | solution.py:514
  155.4 2.5 %shard_map.138 = (bf16[256,1024]{1,0:T(8,128)(2,1)}, bf16[256,1024]{1,0:T(8,128)(2,1)}, f32[32,1024]{1,0:T(8,128)}, f32[32,1024]{1,0:T(8,128)}, bf16[32,4096]{1,0:T(8,128)(2,1)}) custom-call(bf16[256,1024]{1,0:T(8,128)(2,1)} %get-tuple-element.15.refs_0_, bf16[256,1024]{1,0:T(8,128)(2,1)} %get-tuple-element.16.refs_1_, ...), custom_call_target="tpu_custom_call" | custom-call | tf_op jit(solution)/shard_map/pallas_call | solution.py:572

commit v2 on v1

--- a/solution.py
+++ b/solution.py
@@ -176,6 +176,13 @@
             partner,
         ).wait_recv()
 
+    g_copies = []
+    for j, target in enumerate(mates()):
+        g_copies.append(
+            remote(gain, gains.at[my_slot], g_sem.at[j], g_sem.at[2 * h - 1 + my_slot], target)
+        )
+        g_copies[-1].start()
+
     away = pl.ds(pl.multiple_of((1 - half) * half_depth, half_depth), half_depth)
     a_copy = remote(hs.at[:, away], a_in.at[d], a_sem.at[0], a_sem.at[1 + d], other_half(0))
 
@@ -198,12 +205,6 @@
         for c in list(range(split, chunks)) + list(range(early)):
             x_copy(c).start()
 
-    g_copies = []
-    for j, target in enumerate(mates()):
-        g_copies.append(
-            remote(gain, gains.at[my_slot], g_sem.at[j], g_sem.at[2 * h - 1 + my_slot], target)
-        )
-        g_copies[-1].start()
     d_copies = []
     for j in range(1, replicas):
         columns = pl.ds(pl.multiple_of(replica_at(j) * own_w, own_w), own_w)

time: 158 us -> 104 us (0.66)
  Pallas kernels: 157 us -> 103 us
    pallas_call x1, Pallas kernels: 155 us -> 100 us  [per_device(): pl.pallas_call(functools.partial(kernel, groups, replicas, width), out_sh...]
where the time goes in v2:
time: 104 us
  Pallas kernels  103 us (99%)
    pallas_call x1, Pallas kernels, per_device(): pl.pallas_call(functools.partial(kernel, groups, replicas, width), out_sh...  100 us
    pallas_call x1, Pallas kernels, per_device(): pl.pallas_call(write_out, out_shape=tuple((jax.ShapeDtypeStruct(a.shape,...  2.52 us

profile of v2, /device:TPU:0, one launch (start us, length us, event | category | flops | bytes accessed | tf_op | source)
XLA Modules:
  0.0 103.6 jit_solution(2271795663075619950)
XLA Ops:
  0.6 100.4 %shard_map.137 = (bf16[256,1024]{1,0:T(8,128)(2,1)}, bf16[256,1024]{1,0:T(8,128)(2,1)}, f32[32,1024]{1,0:T(8,128)}, f32[32,1024]{1,0:T(8,128)}, bf16[32,4096]{1,0:T(8,128)(2,1)}) custom-call(bf16[256,4096]{1,0:T(8,128)(2,1)} %bitcast.8, bf16[1,512]{1,0:T(2,128)(2,1)} %gain.1, bf16[512,1024]{1,0:T(8,128)(2,1)} %bitcast.9, bf16[512,1024]{1,0:T(8,128)(2,1)} %bitcast.10, ...), custom_call_target="tpu_custom_call" | custom-call | tf_op jit(solution)/shard_map/pallas_call | solution.py:515
  101.0 2.5 %shard_map.138 = (bf16[256,1024]{1,0:T(8,128)(2,1)}, bf16[256,1024]{1,0:T(8,128)(2,1)}, f32[32,1024]{1,0:T(8,128)}, f32[32,1024]{1,0:T(8,128)}, bf16[32,4096]{1,0:T(8,128)(2,1)}) custom-call(bf16[256,1024]{1,0:T(8,128)(2,1)} %get-tuple-element.15.refs_0_, bf16[256,1024]{1,0:T(8,128)(2,1)} %get-tuple-element.16.refs_1_, ...), custom_call_target="tpu_custom_call" | custom-call | tf_op jit(solution)/shard_map/pallas_call | solution.py:573

commit v3 on v2

--- a/solution.py
+++ b/solution.py
@@ -39,12 +39,11 @@
 def kernel(
     groups, replicas, width,
     hs, gain, kw, vw, cosine_in, sine_in, deltas, outer_in, momentum_in, local_in,
-    keys_out, values_out, momentum_out, outer_out, local_out,
+    keys, values, momentum_new, outer_new, local_new,
     cosine, sine, deltas_own, outer, momentum, local,
-    keys, values, momentum_new, outer_new, local_new,
     hs_v, gains, a_in, a_scaled, a_own, weights, inv, acc, c_out, c_in, d_in, o_in,
     hs_sem, g_sem, a_sem, own_sem, w_recv, x_send, z_send, f_send, e_send,
-    c_send, c_recv, d_sem, o_sem, load_sem, store_sem,
+    c_send, c_recv, d_sem, o_sem, load_sem,
 ):
     h = groups // 2
     r, f = lax.axis_index("replica"), lax.axis_index("fsdp")
@@ -111,10 +110,13 @@
         )
 
     mine = pl.ds(pl.multiple_of(r * own_w, own_w), own_w)
-    hs_copy = pltpu.make_async_copy(hs, hs_v, hs_sem)
+    hs_copy = pltpu.make_async_copy(hs, hs_v, hs_sem.at[0])
     hs_copy.start()
     my_slot = slot(d, x)
     partner_slot = slot(d, 1 - x)
+
+    gain_copy = pltpu.make_async_copy(gain, gains.at[my_slot], hs_sem.at[1])
+    gain_copy.start()
 
     def rows(q):
         return pl.ds(pl.multiple_of(q * depth, depth), depth)
@@ -142,6 +144,7 @@
         )
     ]
 
+    hs_copy.wait()
     pl.semaphore_wait(
         barrier, (2 * h - 1) + 1 + (replicas - 1) + jnp.where(is_inner, h, 0)
     )
@@ -184,7 +187,7 @@
         g_copies[-1].start()
 
     away = pl.ds(pl.multiple_of((1 - half) * half_depth, half_depth), half_depth)
-    a_copy = remote(hs.at[:, away], a_in.at[d], a_sem.at[0], a_sem.at[1 + d], other_half(0))
+    a_copy = remote(hs_v.at[:, away], a_in.at[d], a_sem.at[0], a_sem.at[1 + d], other_half(0))
 
     @pl.when(is_inner)
     def _():
@@ -218,7 +221,6 @@
     for copy in loads:
         copy.start()
 
-    hs_copy.wait()
     total = jnp.zeros((tokens, 1), jnp.float32)
     part_w = 2 * depth
     for k in range(features // part_w):
@@ -226,7 +228,7 @@
         total += jnp.sum(part * part, axis=1, keepdims=True)
     inv[...] = jnp.broadcast_to(lax.rsqrt(total / features + 1e-05), inv.shape)
 
-    gains[my_slot] = gain[...]
+    gain_copy.wait()
     for j in range(1, 2 * h):
         q = lax.rem(my_slot + j, 2 * h)
         remote(gain, gains.at[q], g_sem.at[0], g_sem.at[2 * h - 1 + q], partner).wait_recv()
@@ -274,8 +276,6 @@
         moved = 0.9 * momentum[...] + avg
         momentum_new[...] = moved
         outer_new[...] = outer[...] - 0.7 * (avg + 0.9 * moved)
-        store(0, momentum_new, momentum_out).start()
-        store(1, outer_new, outer_out).start()
         for j in range(1, replicas):
             o_copy(j).start()
 
@@ -292,20 +292,12 @@
             local_new[:, theirs] = (
                 part * local[:, theirs].astype(jnp.float32) + part * o_in[j - 1]
             ).astype(jnp.bfloat16)
-        store(2, local_new, local_out).start()
 
     def o_copy(j):
         return remote(
             outer_new, o_in.at[j - 1], o_sem.at[0, j - 1], o_sem.at[1, j - 1],
             {"replica": replica_at(j)},
         )
-
-    def store(i, src, dst):
-        return pltpu.make_async_copy(src, dst, store_sem.at[i])
-
-    def result_copy(src, dst, c, sem):
-        at = pl.ds(pl.multiple_of(c * width, width), width)
-        return pltpu.make_async_copy(src.at[:, at], dst.at[:, at], store_sem.at[sem])
 
     @pl.when(is_inner)
     def _():
@@ -378,7 +370,7 @@
                 for k in range(split, chunks):
                     x_copy(k).start()
             rest(c, False)
-            for i in range(h):
+            for i in reversed(range(h)):
                 away_product(i, c)
             own_product(c)
 
@@ -438,13 +430,11 @@
             turned = head * cosine[...] + pltpu.roll(head, HEAD // 2, 1) * sine[...]
             at = pl.ds(pl.multiple_of(c * width + k * HEAD, HEAD), HEAD)
             keys[:, at] = turned.astype(jnp.bfloat16)
-        result_copy(keys, keys_out, c, 3 + c).start()
 
     @pl.loop(0, per_weight)
     def _(c):
         at = pl.ds(pl.multiple_of(c * width, width), width)
         values[:, at] = summed(c + per_weight).astype(jnp.bfloat16)
-        result_copy(values, values_out, c, 3 + per_weight + c).start()
 
     a_copy.wait_send()
     for copy in g_copies + d_copies:
@@ -484,15 +474,6 @@
                 f_copy(c, j, dist).wait_send()
             for c in range(split, chunks) if inner else range(early):
                 e_copy(c, j, dist).wait_send()
-
-    store(0, momentum_new, momentum_out).wait()
-    store(1, outer_new, outer_out).wait()
-    store(2, local_new, local_out).wait()
-
-    @pl.loop(0, per_weight)
-    def _(c):
-        result_copy(keys, keys_out, c, 3 + c).wait()
-        result_copy(values, values_out, c, 3 + per_weight + c).wait()
 
 
 def per_device(
@@ -515,23 +496,18 @@
     results = pl.pallas_call(
         functools.partial(kernel, groups, replicas, width),
         out_shape=(
-            jax.ShapeDtypeStruct((tokens, kv), bf16),
-            jax.ShapeDtypeStruct((tokens, kv), bf16),
-            jax.ShapeDtypeStruct(own, f32),
-            jax.ShapeDtypeStruct(own, f32),
-            jax.ShapeDtypeStruct(local_params.shape[1:], bf16),
+            pltpu.VMEM((tokens, kv), bf16),
+            pltpu.VMEM((tokens, kv), bf16),
+            pltpu.VMEM(own, f32),
+            pltpu.VMEM(own, f32),
+            pltpu.VMEM(local_params.shape[1:], bf16),
         ),
-        in_specs=[hbm, vmem] + [hbm] * 8,
-        out_specs=[hbm] * 5,
+        in_specs=[hbm] * 10,
+        out_specs=[vmem] * 5,
         scratch_shapes=[
             pltpu.VMEM(cosine.shape, f32),
             pltpu.VMEM(sine.shape, f32),
             pltpu.VMEM(own, f32),
-            pltpu.VMEM(own, f32),
-            pltpu.VMEM(own, f32),
-            pltpu.VMEM(local_params.shape[1:], bf16),
-            pltpu.VMEM((tokens, kv), bf16),
-            pltpu.VMEM((tokens, kv), bf16),
             pltpu.VMEM(own, f32),
             pltpu.VMEM(own, f32),
             pltpu.VMEM(local_params.shape[1:], bf16),
@@ -547,7 +523,7 @@
             pltpu.VMEM((chunks, tokens, width), bf16),
             pltpu.VMEM((replicas - 1,) + own, f32),
             pltpu.VMEM((replicas - 1,) + own, f32),
-            dma,
+            dma((2,)),
             dma((4 * h - 1,)),
             dma((1 + h,)),
             dma((chunks,)),
@@ -561,7 +537,6 @@
             dma((2, replicas - 1)),
             dma((2, replicas - 1)),
             dma((6,)),
-            dma((3 + chunks,)),
         ],
         compiler_params=pltpu.CompilerParams(
             collective_id=0, has_side_effects=True, vmem_limit_bytes=60 * 1024 * 1024
@@ -576,7 +551,7 @@
         in_specs=[vmem] * 5,
         out_specs=[hbm] * 5,
         scratch_shapes=[dma((5,))],
-        compiler_params=pltpu.CompilerParams(vmem_limit_bytes=60 * 1024 * 1024),
+        compiler_params=pltpu.CompilerParams(vmem_limit_bytes=1024 * 1024),
     )(*results)
     return keys[None], values[None], momentum_new, outer_new, local_new[None]
 

time: 104 us -> 99.3 us (0.955)
  Pallas kernels: 103 us -> 98 us
    pallas_call x1, Pallas kernels: 100 us -> 96.8 us  [per_device(): pl.pallas_call(functools.partial(kernel, groups, replicas, width), out_sh...]
    pallas_call x1, Pallas kernels: 2.52 us -> 1.18 us  [per_device(): pl.pallas_call(write_out, out_shape=tuple((jax.ShapeDtypeStruct(a.shape,...]
where the time goes in v3:
time: 99.3 us; the launch traced here: 98.6 us
  Pallas kernels  98 us (99%)
    pallas_call x1, Pallas kernels, per_device(): pl.pallas_call(functools.partial(kernel, groups, replicas, width), out_sh...  96.8 us

profile of v3, /device:TPU:0, one launch (start us, length us, event | category | flops | bytes accessed | tf_op | source)
XLA Modules:
  0.0 98.6 jit_solution(5060925190749946204)
XLA Ops:
  0.6 96.8 %shard_map.137 = (bf16[256,1024]{1,0:T(8,128)(2,1)S(1)}, bf16[256,1024]{1,0:T(8,128)(2,1)S(1)}, f32[32,1024]{1,0:T(8,128)S(1)}, f32[32,1024]{1,0:T(8,128)S(1)}, bf16[32,4096]{1,0:T(8,128)(2,1)S(1)}) custom-call(bf16[256,4096]{1,0:T(8,128)(2,1)} %bitcast.8, bf16[1,512]{1,0:T(2,128)(2,1)} %gain.1, bf16[512,1024]{1,0:T(8,128)(2,1)} %bitcast.9, ...), custom_call_target="tpu_custom_call" | custom-call | tf_op jit(solution)/shard_map/pallas_call | solution.py:496
  97.5 1.2 %shard_map.138 = (bf16[256,1024]{1,0:T(8,128)(2,1)}, bf16[256,1024]{1,0:T(8,128)(2,1)}, f32[32,1024]{1,0:T(8,128)}, f32[32,1024]{1,0:T(8,128)}, bf16[32,4096]{1,0:T(8,128)(2,1)}) custom-call(bf16[256,1024]{1,0:T(8,128)(2,1)S(1)} %get-tuple-element.15.refs_0_, bf16[256,1024]{1,0:T(8,128)(2,1)S(1)} %get-tuple-element.16.refs_1_, ...), custom_call_target="tpu_custom_call" | custom-call | tf_op jit(solution)/shard_map/pallas_call | solution.py:548

commit v4 on v3

v4 whole, which is shorter than its diff:
```python
import functools

import jax
import jax.numpy as jnp
import numpy as np
from jax import lax
from jax.experimental import pallas as pl
from jax.experimental.pallas import tpu as pltpu
from jax.sharding import PartitionSpec as P

HEAD = 128
MESH = pl.DeviceIdType.MESH


def rotation_tables(tokens, head_size):
    half_width = head_size // 2
    exponent = np.arange(half_width, dtype=np.float32) * np.float32(2.0 / head_size)
    frequency = np.power(np.float32(500000.0), -exponent)
    angles = np.arange(tokens, dtype=np.float32)[:, None] * frequency[None, :]
    cosine, sine = np.cos(angles), np.sin(angles)
    return (
        jnp.asarray(np.concatenate([cosine, cosine], axis=1)),
        jnp.asarray(np.concatenate([-sine, sine], axis=1)),
    )


def write_out(*refs):
    count = len(refs) // 2
    sems = refs[-1]
    copies = [
        pltpu.make_async_copy(refs[i], refs[count + i], sems.at[i]) for i in range(count)
    ]
    for copy in copies:
        copy.start()
    for copy in copies:
        copy.wait()


def kernel(
    groups, replicas, width,
    hs, gain, kw, vw, cosine_in, sine_in, deltas, outer_in, momentum_in, local_in,
    keys, values, momentum_new, outer_new, local_new,
    rotation, state, local,
    hs_v, gains, a_in, a_scaled, a_own, weights, inv, acc, c_out, c_in, d_in, o_in,
    hs_sem, g_sem, g_recv, a_sem, z_recv, p_recv, w_recv, x_send, z_send, f_send, e_send,
    c_send, c_recv, d_sem, o_sem, load_sem,
):
    h = groups // 2
    r, f = lax.axis_index("replica"), lax.axis_index("fsdp")
    x, g = lax.rem(f, 2), lax.div(f, 2)
    half = lax.div(g, h)
    local_g = lax.rem(g, h)
    d = (h - 1 - local_g) * (1 - half) + local_g * half
    tokens, depth = hs.shape[0], kw.shape[0]
    half_depth = 2 * h * depth
    per_weight = kw.shape[1] // width
    chunks = 2 * per_weight
    first = chunks // 2
    split = chunks - chunks // 4
    early = chunks // 4
    own_w = outer_in.shape[1]
    cosine, sine = rotation.at[0], rotation.at[1]
    deltas_own, outer, momentum = state.at[0], state.at[1], state.at[2]
    features = hs.shape[1]

    def place(dist):
        return (h - 1 - dist) * (1 - half) + dist * half

    def slot(dist, side):
        return 2 * place(dist) + side

    def device(dist, side):
        return {"fsdp": 2 * (half * h + place(dist)) + side}

    def other_half(dist):
        return {"fsdp": 2 * ((1 - half) * (h + dist) + half * (h - 1 - dist)) + x}

    partner = device(d, 1 - x)
    outer_peers = [(0, True)] + [(1 + lax.rem(d - 1 + j, h - 1), False) for j in range(1, h - 1)]
    inner_peers = [(j, False) for j in range(1, h)]
    is_inner = d == 0

    def replica_at(j):
        return lax.rem(r + j, replicas)

    barrier = pltpu.get_barrier_semaphore()

    def greet(target):
        pl.semaphore_signal(barrier, inc=1, device_id=target, device_id_type=MESH)

    greet(partner)
    for j in range(1, replicas):
        greet({"replica": replica_at(j)})

    @pl.when(is_inner)
    def _():
        for i in range(h):
            greet(other_half(i))
        for dist, _ in inner_peers:
            greet(device(dist, x))

    @pl.when(jnp.logical_not(is_inner))
    def _():
        for dist, _ in outer_peers:
            greet(device(dist, x))

    def remote(src, dst, send, recv, target):
        return pltpu.make_async_remote_copy(
            src_ref=src, dst_ref=dst, send_sem=send, recv_sem=recv,
            device_id=target, device_id_type=MESH,
        )

    mine = pl.ds(pl.multiple_of(r * own_w, own_w), own_w)
    away = pl.ds(pl.multiple_of((1 - half) * half_depth, half_depth), half_depth)
    home = pl.ds(pl.multiple_of(half * half_depth, half_depth), half_depth)
    hs_copy = pltpu.make_async_copy(hs.at[:, away], hs_v.at[:, away], hs_sem.at[0])
    hs_copy.start()
    home_copy = pltpu.make_async_copy(hs.at[:, home], hs_v.at[:, home], hs_sem.at[1])
    my_slot = slot(d, x)
    partner_slot = slot(d, 1 - x)

    def rows(q):
        return pl.ds(pl.multiple_of(q * depth, depth), depth)

    def source(c):
        return (kw if c < per_weight else vw).at[:, pl.ds((c % per_weight) * width, width)]

    own_copies = [
        pltpu.make_async_copy(source(c), weights.at[c, rows(my_slot)], w_recv.at[c])
        for c in range(chunks)
    ]
    loads = [
        pltpu.make_async_copy(src, dst, load_sem.at[i])
        for i, src, dst in (
            (0, deltas.at[:, mine], deltas_own),
            (0, outer_in, outer),
            (0, momentum_in, momentum),
            (1, cosine_in, cosine),
            (1, sine_in, sine),
            (2, local_in, local),
        )
    ]

    hs_copy.wait()
    pl.semaphore_wait(barrier, 1 + (h - 1) + 1 + (replicas - 1))

    def heard(sender, receiver):
        return lax.rem(sender - receiver - 1 + h, h)

    def x_copy(c, known):
        arrival = w_recv.at[c] if known is None else p_recv.at[known]
        return remote(source(c), weights.at[c, rows(my_slot)], x_send, arrival, partner)

    def z_copy(c, j, dist):
        return remote(
            source(c), weights.at[c, rows(my_slot)], z_send.at[j], z_recv.at[heard(d, dist), c],
            device(dist, x),
        )

    def f_copy(c, j, dist):
        at = weights.at[c, rows(slot(dist, x))]
        return remote(at, at, f_send.at[j], w_recv.at[c], partner)

    def e_copy(c, j, dist):
        at = weights.at[c, rows(partner_slot)]
        return remote(at, at, e_send.at[j], w_recv.at[c], device(dist, x))

    def landed(ref, sem):
        remote(ref, ref, x_send, sem, partner).wait_recv()

    def left(ref, sem):
        remote(ref, ref, sem, w_recv.at[0], partner).wait_send()

    def from_peer(c, dist):
        landed(weights.at[c, rows(slot(dist, x))], z_recv.at[heard(dist, d), c])

    def from_partner(c, known):
        landed(weights.at[c, rows(partner_slot)], p_recv.at[known])

    def rest(c, known):
        count = h if known else h + 1
        landed(weights.at[c, pl.ds(0, count * depth)], w_recv.at[c])

    def send_gain(peers):
        remote(gain, gains.at[my_slot], g_sem, g_recv.at[h - 1], partner).start()
        for dist, _ in peers:
            remote(
                gain, gains.at[my_slot], g_sem, g_recv.at[heard(d, dist)], device(dist, x)
            ).start()

    def pass_gain(peers):
        for dist, _ in peers:
            at = gains.at[slot(dist, x)]
            landed(at, g_recv.at[heard(dist, d)])
            remote(at, at, g_sem, g_recv.at[h - 1], partner).start()

    a_copy = remote(hs_v.at[:, away], a_in.at[d], a_sem.at[0], a_sem.at[1 + d], other_half(0))

    @pl.when(is_inner)
    def _():
        a_copy.start()
        send_gain(inner_peers)
        for c in range(2):
            x_copy(c, c if c < early else None).start()
        for c in range(chunks):
            for j, (dist, _) in enumerate(inner_peers):
                z_copy(c, j, dist).start()

    @pl.when(jnp.logical_not(is_inner))
    def _():
        send_gain(outer_peers)
        for c in range(chunks):
            if c == first:
                a_copy.start()
            for j, (dist, _) in enumerate(outer_peers):
                z_copy(c, j, dist).start()
        for c in list(range(split, chunks)) + list(range(early)):
            x_copy(c, c - split if c >= split else None).start()

    gain_copy = pltpu.make_async_copy(gain, gains.at[my_slot], g_recv.at[h - 1])
    gain_copy.start()
    home_copy.start()
    for j in range(1, replicas):
        columns = pl.ds(pl.multiple_of(replica_at(j) * own_w, own_w), own_w)
        remote(
            deltas.at[:, columns], d_in.at[j - 1], d_sem.at[0], d_sem.at[1],
            {"replica": replica_at(j)},
        ).start()
    for copy in loads + own_copies:
        copy.start()

    home_copy.wait()
    total = jnp.zeros((tokens, 1), jnp.float32)
    part_w = 2 * depth
    for k in range(features // part_w):
        part = hs_v[:, k * part_w : (k + 1) * part_w].astype(jnp.float32)
        total += jnp.sum(part * part, axis=1, keepdims=True)
    inv[...] = jnp.broadcast_to(lax.rsqrt(total / features + 1e-05), inv.shape)

    @pl.when(is_inner)
    def _():
        pass_gain(inner_peers)

    @pl.when(jnp.logical_not(is_inner))
    def _():
        pass_gain(outer_peers)

    landed(gains.at[pl.ds(0, h + 1)], g_recv.at[h - 1])

    def scale(target, origin, base):
        for q in range(2 * h):
            at = pl.ds(base + q * depth, depth)
            target[:, q * depth : (q + 1) * depth] = (
                origin[:, at].astype(jnp.float32) * gains[q].astype(jnp.float32)
            ).astype(jnp.bfloat16)

    @pl.when(half == 0)
    def _():
        scale(a_own, hs_v, 0)

    @pl.when(half == 1)
    def _():
        scale(a_own, hs_v, half_depth)

    def own_product(c):
        acc[c] = jnp.dot(a_own[...], weights[c], preferred_element_type=jnp.float32)

    def away_product(i, c, final=False):
        c_out[i, c] = jnp.dot(
            a_scaled[i], weights[c], preferred_element_type=jnp.float32
        ).astype(jnp.bfloat16)
        remote(
            c_out.at[i, c], c_in.at[c], c_send, c_recv.at[1 if final else 0], other_half(i)
        ).start()

    def outer_step():
        pltpu.make_async_copy(state, state, load_sem.at[0]).wait()
        landed(d_in, d_sem.at[1])
        avg = deltas_own[...]
        for j in range(1, replicas):
            avg += d_in[j - 1]
        avg = avg / replicas
        moved = 0.9 * momentum[...] + avg
        momentum_new[...] = moved
        outer_new[...] = outer[...] - 0.7 * (avg + 0.9 * moved)
        for j in range(1, replicas):
            remote(
                outer_new, o_in.at[j - 1], o_sem.at[0], o_sem.at[1], {"replica": replica_at(j)}
            ).start()

    def merge_step():
        part = jnp.float32(0.5)
        loads[-1].wait()
        local_new[:, mine] = (
            part * local[:, mine].astype(jnp.float32) + part * outer_new[...]
        ).astype(jnp.bfloat16)
        landed(o_in, o_sem.at[1])
        for j in range(1, replicas):
            theirs = pl.ds(
                pl.multiple_of(lax.rem(r + replicas - j, replicas) * own_w, own_w), own_w
            )
            local_new[:, theirs] = (
                part * local[:, theirs].astype(jnp.float32) + part * o_in[j - 1]
            ).astype(jnp.bfloat16)

    @pl.when(is_inner)
    def _():
        def pass_on(c):
            for j, (dist, _) in enumerate(inner_peers):
                from_peer(c, dist)
                if c < split:
                    f_copy(c, j, dist).start()

        for c in range(first):
            pass_on(c)
            if c + 2 < first:
                x_copy(c + 2, None).start()
            if c < early:
                from_partner(c, c)
                for j, (dist, _) in enumerate(inner_peers):
                    e_copy(c, j, dist).start()
            if c == 0:
                outer_step()
            if c == 1:
                merge_step()
        for c in range(first, split):
            x_copy(c, None).start()

        remote(hs.at[:, away], a_in.at[0], a_sem.at[0], a_sem.at[1], partner).wait_recv()
        for q in range(2 * h):
            at = slice(q * depth, (q + 1) * depth)
            a_scaled[0, :, at] = (
                a_in[0, :, at].astype(jnp.float32) * gains[q].astype(jnp.float32)
            ).astype(jnp.bfloat16)

        @pl.loop(0, early)
        def _(c):
            rest(c, True)
            away_product(0, c)
            own_product(c)

        @pl.loop(early, first)
        def _(c):
            rest(c, False)
            away_product(0, c)
            own_product(c)

        for i in range(1, h):
            remote(
                hs.at[:, away], a_in.at[i], a_sem.at[0], a_sem.at[1 + i], partner
            ).wait_recv()
            for q in range(2 * h):
                at = slice(q * depth, (q + 1) * depth)
                a_scaled[i, :, at] = (
                    a_in[i, :, at].astype(jnp.float32) * gains[q].astype(jnp.float32)
                ).astype(jnp.bfloat16)

            @pl.loop(0, first)
            def _(c):
                away_product(i, c)

        pass_on(first)
        for c in range(first, chunks):
            if c + 1 < chunks:
                pass_on(c + 1)
            if c + 1 == split - 1:
                for k in range(split, chunks):
                    x_copy(k, None).start()
            rest(c, False)
            for i in reversed(range(h)):
                away_product(i, c, c == chunks - 1)
            own_product(c)

    @pl.when(jnp.logical_not(is_inner))
    def _():
        for c in range(chunks):
            for j, (dist, _) in enumerate(outer_peers):
                from_peer(c, dist)
                if c >= early:
                    f_copy(c, j, dist).start()
            if early <= c < split:
                x_copy(c, None).start()
            if c == 1:
                for k in range(split, chunks):
                    from_partner(k, k - split)
                    for j, (dist, inner) in enumerate(outer_peers):
                        if inner:
                            e_copy(k, j, dist).start()
                outer_step()
            if c == 2:
                merge_step()

        def finish(c, known):
            rest(c, known)
            own_product(c)

        @pl.loop(0, split)
        def _(c):
            finish(c, False)

        @pl.loop(split, chunks)
        def _(c):
            finish(c, True)

    landed(rotation, load_sem.at[1])

    def summed(c):
        return (acc[c] + c_in[c].astype(jnp.float32)) * inv[:, 0:1]

    landed(c_in.at[pl.ds(0, chunks - 1)], c_recv.at[0])

    @pl.loop(0, per_weight)
    def _(c):
        value = summed(c)
        for k in range(width // HEAD):
            head = value[:, k * HEAD : (k + 1) * HEAD]
            turned = head * cosine[...] + pltpu.roll(head, HEAD // 2, 1) * sine[...]
            at = pl.ds(pl.multiple_of(c * width + k * HEAD, HEAD), HEAD)
            keys[:, at] = turned.astype(jnp.bfloat16)

    @pl.loop(0, per_weight - 1)
    def _(c):
        at = pl.ds(pl.multiple_of(c * width, width), width)
        values[:, at] = summed(c + per_weight).astype(jnp.bfloat16)

    a_copy.wait_send()
    left(d_in, d_sem.at[0])
    left(o_in, o_sem.at[0])
    left(gains.at[pl.ds(0, 2 * h - 1)], g_sem)
    left(weights.at[:, rows(my_slot)], x_send)
    for j in range(h - 1):
        left(weights.at[:, rows(my_slot)], z_send.at[j])
        left(weights.at[pl.ds(0, split), rows(my_slot)], f_send.at[j])

    @pl.when(is_inner)
    def _():
        for j in range(h - 1):
            left(weights.at[pl.ds(0, early), rows(my_slot)], e_send.at[j])

    @pl.when(jnp.logical_not(is_inner))
    def _():
        left(weights.at[pl.ds(0, early), rows(my_slot)], e_send.at[0])

    landed(c_in.at[chunks - 1], c_recv.at[1])
    values[:, pl.ds((per_weight - 1) * width, width)] = summed(chunks - 1).astype(jnp.bfloat16)

    @pl.when(is_inner)
    def _():
        left(c_out, c_send)


def per_device(
    groups, replicas,
    hidden_states, norm_gain, key_weight, value_weight, deltas, outer_params, momentum, local_params,
):
    hs, kw, vw = hidden_states[0], key_weight[0], value_weight[0]
    tokens, features = hs.shape
    depth, kv = kw.shape
    width = 2 * HEAD
    chunks = 2 * kv // width
    h = groups // 2
    half_depth = groups * depth
    cosine, sine = rotation_tables(tokens, HEAD)
    own = outer_params.shape
    vmem = pl.BlockSpec(memory_space=pltpu.VMEM)
    hbm = pl.BlockSpec(memory_space=pl.ANY)
    dma = pltpu.SemaphoreType.DMA
    bf16, f32 = jnp.bfloat16, jnp.float32
    results = pl.pallas_call(
        functools.partial(kernel, groups, replicas, width),
        out_shape=(
            pltpu.VMEM((tokens, kv), bf16),
            pltpu.VMEM((tokens, kv), bf16),
            pltpu.VMEM(own, f32),
            pltpu.VMEM(own, f32),
            pltpu.VMEM(local_params.shape[1:], bf16),
        ),
        in_specs=[hbm] * 10,
        out_specs=[vmem] * 5,
        scratch_shapes=[
            pltpu.VMEM((2, tokens, HEAD), f32),
            pltpu.VMEM((3,) + own, f32),
            pltpu.VMEM(local_params.shape[1:], bf16),
            pltpu.VMEM((tokens, features), bf16),
            pltpu.VMEM((2 * h, 1, depth), bf16),
            pltpu.VMEM((h, tokens, half_depth), bf16),
            pltpu.VMEM((h, tokens, half_depth), bf16),
            pltpu.VMEM((tokens, half_depth), bf16),
            pltpu.VMEM((chunks, half_depth, width), bf16),
            pltpu.VMEM((tokens, HEAD), f32),
            pltpu.VMEM((chunks, tokens, width), f32),
            pltpu.VMEM((h, chunks, tokens, width), bf16),
            pltpu.VMEM((chunks, tokens, width), bf16),
            pltpu.VMEM((replicas - 1,) + own, f32),
            pltpu.VMEM((replicas - 1,) + own, f32),
            dma((2,)),
            dma,
            dma((h,)),
            dma((1 + h,)),
            dma((h - 1, chunks)),
            dma((chunks // 4,)),
            dma((chunks,)),
            dma,
            dma((h - 1,)),
            dma((h - 1,)),
            dma((h - 1,)),
            dma,
            dma((2,)),
            dma((2,)),
            dma((2,)),
            dma((3,)),
        ],
        compiler_params=pltpu.CompilerParams(
            collective_id=0, has_side_effects=True, vmem_limit_bytes=60 * 1024 * 1024
        ),
    )(
        hs, norm_gain, kw, vw, cosine, sine,
        deltas[0], outer_params, momentum, local_params[0],
    )
    keys, values, momentum_new, outer_new, local_new = pl.pallas_call(
        write_out,
        out_shape=tuple(jax.ShapeDtypeStruct(a.shape, a.dtype) for a in results),
        in_specs=[vmem] * 5,
        out_specs=[hbm] * 5,
        scratch_shapes=[dma((5,))],
        compiler_params=pltpu.CompilerParams(vmem_limit_bytes=1024 * 1024),
    )(*results)
    return keys[None], values[None], momentum_new, outer_new, local_new[None]


def solution(mesh):
    in_specs = (
        P("replica", "fsdp", None),
        P("replica", "fsdp"),
        P("replica", "fsdp", None),
        P("replica", "fsdp", None),
        P("replica", "fsdp", None),
        P("fsdp", "replica"),
        P("fsdp", "replica"),
        P("replica", "fsdp", None),
    )
    out_specs = (
        P("replica", "fsdp", None),
        P("replica", "fsdp", None),
        P("fsdp", "replica"),
        P("fsdp", "replica"),
        P("replica", "fsdp", None),
    )
    groups, replicas = mesh.shape["fsdp"] // 2, mesh.shape["replica"]
    return jax.shard_map(
        functools.partial(per_device, groups, replicas),
        mesh=mesh, in_specs=in_specs, out_specs=out_specs, check_vma=False,
    )
```

time: 99.3 us -> 98 us (0.987)
  Pallas kernels: 98 us -> 96.7 us
    pallas_call x1, Pallas kernels: 96.8 us -> 95.6 us  [per_device(): pl.pallas_call(functools.partial(kernel, groups, replicas, width), out_sh...]
where the time goes in v4:
time: 98 us; the launch traced here: 97.4 us
  Pallas kernels  96.7 us (99%)
    pallas_call x1, Pallas kernels, per_device(): pl.pallas_call(functools.partial(kernel, groups, replicas, width), out_sh...  95.6 us

profile of v4, /device:TPU:0, one launch (start us, length us, event | category | flops | bytes accessed | tf_op | source)
XLA Modules:
  0.0 97.4 jit_solution(11232657218864975555)
XLA Ops:
  0.6 95.6 %shard_map.137 = (bf16[256,1024]{1,0:T(8,128)(2,1)S(1)}, bf16[256,1024]{1,0:T(8,128)(2,1)S(1)}, f32[32,1024]{1,0:T(8,128)S(1)}, f32[32,1024]{1,0:T(8,128)S(1)}, bf16[32,4096]{1,0:T(8,128)(2,1)S(1)}) custom-call(bf16[256,4096]{1,0:T(8,128)(2,1)} %bitcast.8, bf16[1,512]{1,0:T(2,128)(2,1)} %gain.1, bf16[512,1024]{1,0:T(8,128)(2,1)} %bitcast.9, ...), custom_call_target="tpu_custom_call" | custom-call | tf_op jit(solution)/shard_map/pallas_call | solution.py:469
  96.2 1.2 %shard_map.138 = (bf16[256,1024]{1,0:T(8,128)(2,1)}, bf16[256,1024]{1,0:T(8,128)(2,1)}, f32[32,1024]{1,0:T(8,128)}, f32[32,1024]{1,0:T(8,128)}, bf16[32,4096]{1,0:T(8,128)(2,1)}) custom-call(bf16[256,1024]{1,0:T(8,128)(2,1)S(1)} %get-tuple-element.15.refs_0_, bf16[256,1024]{1,0:T(8,128)(2,1)S(1)} %get-tuple-element.16.refs_1_, ...), custom_call_target="tpu_custom_call" | custom-call | tf_op jit(solution)/shard_map/pallas_call | solution.py:520

commit v5 on v4

--- a/solution.py
+++ b/solution.py
@@ -40,7 +40,7 @@
     groups, replicas, width,
     hs, gain, kw, vw, cosine_in, sine_in, deltas, outer_in, momentum_in, local_in,
     keys, values, momentum_new, outer_new, local_new,
-    rotation, state, local,
+    rotation, state, local, lead,
     hs_v, gains, a_in, a_scaled, a_own, weights, inv, acc, c_out, c_in, d_in, o_in,
     hs_sem, g_sem, g_recv, a_sem, z_recv, p_recv, w_recv, x_send, z_send, f_send, e_send,
     c_send, c_recv, d_sem, o_sem, load_sem,
@@ -55,7 +55,7 @@
     half_depth = 2 * h * depth
     per_weight = kw.shape[1] // width
     chunks = 2 * per_weight
-    first = chunks // 2
+    first = chunks // 2 - 1
     split = chunks - chunks // 4
     early = chunks // 4
     own_w = outer_in.shape[1]
@@ -94,8 +94,7 @@
 
     @pl.when(is_inner)
     def _():
-        for i in range(h):
-            greet(other_half(i))
+        greet(other_half(0))
         for dist, _ in inner_peers:
             greet(device(dist, x))
 
@@ -115,6 +114,8 @@
     home = pl.ds(pl.multiple_of(half * half_depth, half_depth), half_depth)
     hs_copy = pltpu.make_async_copy(hs.at[:, away], hs_v.at[:, away], hs_sem.at[0])
     hs_copy.start()
+    lead_copy = pltpu.make_async_copy(kw.at[:, pl.ds(0, width)], lead, hs_sem.at[2])
+    lead_copy.start()
     home_copy = pltpu.make_async_copy(hs.at[:, home], hs_v.at[:, home], hs_sem.at[1])
     my_slot = slot(d, x)
     partner_slot = slot(d, 1 - x)
@@ -126,7 +127,7 @@
         return (kw if c < per_weight else vw).at[:, pl.ds((c % per_weight) * width, width)]
 
     own_copies = [
-        pltpu.make_async_copy(source(c), weights.at[c, rows(my_slot)], w_recv.at[c])
+        pltpu.make_async_copy(source(c), weights.at[c, rows(my_slot)], hs_sem.at[3])
         for c in range(chunks)
     ]
     loads = [
@@ -141,19 +142,21 @@
         )
     ]
 
-    hs_copy.wait()
-    pl.semaphore_wait(barrier, 1 + (h - 1) + 1 + (replicas - 1))
+    for copy in own_copies:
+        copy.start()
+    pl.semaphore_wait(barrier, 1 + (h - 1) + (replicas - 1) + jnp.where(is_inner, 1, 0))
 
     def heard(sender, receiver):
         return lax.rem(sender - receiver - 1 + h, h)
 
     def x_copy(c, known):
         arrival = w_recv.at[c] if known is None else p_recv.at[known]
-        return remote(source(c), weights.at[c, rows(my_slot)], x_send, arrival, partner)
+        at = weights.at[c, rows(my_slot)]
+        return remote(lead if c == 0 else at, at, x_send, arrival, partner)
 
     def z_copy(c, j, dist):
         return remote(
-            source(c), weights.at[c, rows(my_slot)], z_send.at[j], z_recv.at[heard(d, dist), c],
+            lead if c == 0 else weights.at[c, rows(my_slot)], weights.at[c, rows(my_slot)], z_send.at[j], z_recv.at[heard(d, dist), c],
             device(dist, x),
         )
 
@@ -178,8 +181,12 @@
         landed(weights.at[c, rows(partner_slot)], p_recv.at[known])
 
     def rest(c, known):
-        count = h if known else h + 1
+        count = h - 1 if known else h
         landed(weights.at[c, pl.ds(0, count * depth)], w_recv.at[c])
+
+    def own_wait():
+        at = weights.at[:, rows(my_slot)]
+        pltpu.make_async_copy(at, at, hs_sem.at[3]).wait()
 
     def send_gain(peers):
         remote(gain, gains.at[my_slot], g_sem, g_recv.at[h - 1], partner).start()
@@ -198,20 +205,25 @@
 
     @pl.when(is_inner)
     def _():
+        send_gain(inner_peers)
+        hs_copy.wait()
         a_copy.start()
-        send_gain(inner_peers)
-        for c in range(2):
-            x_copy(c, c if c < early else None).start()
+        lead_copy.wait()
         for c in range(chunks):
+            if c == 1:
+                own_wait()
+            if c < 2:
+                x_copy(c, c if c < early else None).start()
             for j, (dist, _) in enumerate(inner_peers):
                 z_copy(c, j, dist).start()
 
     @pl.when(jnp.logical_not(is_inner))
     def _():
         send_gain(outer_peers)
-        for c in range(chunks):
-            if c == first:
-                a_copy.start()
+        lead_copy.wait()
+        for c in range(first):
+            if c == 1:
+                own_wait()
             for j, (dist, _) in enumerate(outer_peers):
                 z_copy(c, j, dist).start()
         for c in list(range(split, chunks)) + list(range(early)):
@@ -226,8 +238,21 @@
             deltas.at[:, columns], d_in.at[j - 1], d_sem.at[0], d_sem.at[1],
             {"replica": replica_at(j)},
         ).start()
-    for copy in loads + own_copies:
+    for copy in loads:
         copy.start()
+
+    @pl.when(is_inner)
+    def _():
+        pass_gain(inner_peers)
+
+    @pl.when(jnp.logical_not(is_inner))
+    def _():
+        pass_gain(outer_peers)
+        hs_copy.wait()
+        a_copy.start()
+        for c in range(first, chunks):
+            for j, (dist, _) in enumerate(outer_peers):
+                z_copy(c, j, dist).start()
 
     home_copy.wait()
     total = jnp.zeros((tokens, 1), jnp.float32)
@@ -237,16 +262,6 @@
         total += jnp.sum(part * part, axis=1, keepdims=True)
     inv[...] = jnp.broadcast_to(lax.rsqrt(total / features + 1e-05), inv.shape)
 
-    @pl.when(is_inner)
-    def _():
-        pass_gain(inner_peers)
-
-    @pl.when(jnp.logical_not(is_inner))
-    def _():
-        pass_gain(outer_peers)
-
-    landed(gains.at[pl.ds(0, h + 1)], g_recv.at[h - 1])
-
     def scale(target, origin, base):
         for q in range(2 * h):
             at = pl.ds(base + q * depth, depth)
@@ -254,13 +269,16 @@
                 origin[:, at].astype(jnp.float32) * gains[q].astype(jnp.float32)
             ).astype(jnp.bfloat16)
 
-    @pl.when(half == 0)
-    def _():
-        scale(a_own, hs_v, 0)
-
-    @pl.when(half == 1)
-    def _():
-        scale(a_own, hs_v, half_depth)
+    def scale_own():
+        landed(gains.at[pl.ds(0, h + 1)], g_recv.at[h - 1])
+
+        @pl.when(half == 0)
+        def _():
+            scale(a_own, hs_v, 0)
+
+        @pl.when(half == 1)
+        def _():
+            scale(a_own, hs_v, half_depth)
 
     def own_product(c):
         acc[c] = jnp.dot(a_own[...], weights[c], preferred_element_type=jnp.float32)
@@ -311,9 +329,17 @@
                 if c < split:
                     f_copy(c, j, dist).start()
 
+        def take(i):
+            landed(a_in.at[i], a_sem.at[1 + i])
+            for q in range(2 * h):
+                at = slice(q * depth, (q + 1) * depth)
+                a_scaled[i, :, at] = (
+                    a_in[i, :, at].astype(jnp.float32) * gains[q].astype(jnp.float32)
+                ).astype(jnp.bfloat16)
+
         for c in range(first):
             pass_on(c)
-            if c + 2 < first:
+            if c + 2 <= first:
                 x_copy(c + 2, None).start()
             if c < early:
                 from_partner(c, c)
@@ -323,37 +349,23 @@
                 outer_step()
             if c == 1:
                 merge_step()
-        for c in range(first, split):
+        for c in range(first + 1, split):
             x_copy(c, None).start()
 
-        remote(hs.at[:, away], a_in.at[0], a_sem.at[0], a_sem.at[1], partner).wait_recv()
-        for q in range(2 * h):
-            at = slice(q * depth, (q + 1) * depth)
-            a_scaled[0, :, at] = (
-                a_in[0, :, at].astype(jnp.float32) * gains[q].astype(jnp.float32)
-            ).astype(jnp.bfloat16)
+        scale_own()
 
         @pl.loop(0, early)
         def _(c):
             rest(c, True)
-            away_product(0, c)
             own_product(c)
 
         @pl.loop(early, first)
         def _(c):
             rest(c, False)
-            away_product(0, c)
             own_product(c)
 
-        for i in range(1, h):
-            remote(
-                hs.at[:, away], a_in.at[i], a_sem.at[0], a_sem.at[1 + i], partner
-            ).wait_recv()
-            for q in range(2 * h):
-                at = slice(q * depth, (q + 1) * depth)
-                a_scaled[i, :, at] = (
-                    a_in[i, :, at].astype(jnp.float32) * gains[q].astype(jnp.float32)
-                ).astype(jnp.bfloat16)
+        for i in reversed(range(h)):
+            take(i)
 
             @pl.loop(0, first)
             def _(c):
@@ -381,20 +393,27 @@
             if early <= c < split:
                 x_copy(c, None).start()
             if c == 1:
-                for k in range(split, chunks):
-                    from_partner(k, k - split)
-                    for j, (dist, inner) in enumerate(outer_peers):
-                        if inner:
-                            e_copy(k, j, dist).start()
                 outer_step()
             if c == 2:
                 merge_step()
 
+        scale_own()
+
         def finish(c, known):
             rest(c, known)
             own_product(c)
 
-        @pl.loop(0, split)
+        @pl.loop(0, early)
+        def _(c):
+            finish(c, False)
+
+        for k in range(split, chunks):
+            from_partner(k, k - split)
+            for j, (dist, inner) in enumerate(outer_peers):
+                if inner:
+                    e_copy(k, j, dist).start()
+
+        @pl.loop(early, split)
         def _(c):
             finish(c, False)
 
@@ -481,6 +500,7 @@
             pltpu.VMEM((2, tokens, HEAD), f32),
             pltpu.VMEM((3,) + own, f32),
             pltpu.VMEM(local_params.shape[1:], bf16),
+            pltpu.VMEM((depth, width), bf16),
             pltpu.VMEM((tokens, features), bf16),
             pltpu.VMEM((2 * h, 1, depth), bf16),
             pltpu.VMEM((h, tokens, half_depth), bf16),
@@ -493,7 +513,7 @@
             pltpu.VMEM((chunks, tokens, width), bf16),
             pltpu.VMEM((replicas - 1,) + own, f32),
             pltpu.VMEM((replicas - 1,) + own, f32),
-            dma((2,)),
+            dma((4,)),
             dma,
             dma((h,)),
             dma((1 + h,)),

time: 98 us -> 97.7 us (level)
  no operation moved by 1% of the time
where the time goes in v5:
time: 97.7 us; the launch traced here: 97.5 us
  Pallas kernels  96.9 us (99%)
    pallas_call x1, Pallas kernels, per_device(): pl.pallas_call(functools.partial(kernel, groups, replicas, width), out_sh...  95.7 us

profile of v5, /device:TPU:0, one launch (start us, length us, event | category | flops | bytes accessed | tf_op | source)
XLA Modules:
  0.0 97.5 jit_solution(3123014453781560876)
XLA Ops:
  0.6 95.7 %shard_map.137 = (bf16[256,1024]{1,0:T(8,128)(2,1)S(1)}, bf16[256,1024]{1,0:T(8,128)(2,1)S(1)}, f32[32,1024]{1,0:T(8,128)S(1)}, f32[32,1024]{1,0:T(8,128)S(1)}, bf16[32,4096]{1,0:T(8,128)(2,1)S(1)}) custom-call(bf16[256,4096]{1,0:T(8,128)(2,1)} %bitcast.8, bf16[1,512]{1,0:T(2,128)(2,1)} %gain.1, bf16[512,1024]{1,0:T(8,128)(2,1)} %bitcast.9, ...), custom_call_target="tpu_custom_call" | custom-call | tf_op jit(solution)/shard_map/pallas_call | solution.py:488
  96.3 1.2 %shard_map.138 = (bf16[256,1024]{1,0:T(8,128)(2,1)}, bf16[256,1024]{1,0:T(8,128)(2,1)}, f32[32,1024]{1,0:T(8,128)}, f32[32,1024]{1,0:T(8,128)}, bf16[32,4096]{1,0:T(8,128)(2,1)}) custom-call(bf16[256,1024]{1,0:T(8,128)(2,1)S(1)} %get-tuple-element.15.refs_0_, bf16[256,1024]{1,0:T(8,128)(2,1)S(1)} %get-tuple-element.16.refs_1_, ...), custom_call_target="tpu_custom_call" | custom-call | tf_op jit(solution)/shard_map/pallas_call | solution.py:540

commit v6 on v5

--- a/solution.py
+++ b/solution.py
@@ -79,6 +79,7 @@
     outer_peers = [(0, True)] + [(1 + lax.rem(d - 1 + j, h - 1), False) for j in range(1, h - 1)]
     inner_peers = [(j, False) for j in range(1, h)]
     is_inner = d == 0
+    late = lax.rem(r, 2) == 0
 
     def replica_at(j):
         return lax.rem(r + j, replicas)
@@ -283,13 +284,15 @@
     def own_product(c):
         acc[c] = jnp.dot(a_own[...], weights[c], preferred_element_type=jnp.float32)
 
-    def away_product(i, c, final=False):
+    def away_send(i, c, final=False):
+        remote(
+            c_out.at[i, c], c_in.at[c], c_send, c_recv.at[1 if final else 0], other_half(i)
+        ).start()
+
+    def away_product(i, c):
         c_out[i, c] = jnp.dot(
             a_scaled[i], weights[c], preferred_element_type=jnp.float32
         ).astype(jnp.bfloat16)
-        remote(
-            c_out.at[i, c], c_in.at[c], c_send, c_recv.at[1 if final else 0], other_half(i)
-        ).start()
 
     def outer_step():
         pltpu.make_async_copy(state, state, load_sem.at[0]).wait()
@@ -370,6 +373,7 @@
             @pl.loop(0, first)
             def _(c):
                 away_product(i, c)
+                away_send(i, c)
 
         pass_on(first)
         for c in range(first, chunks):
@@ -380,7 +384,13 @@
                     x_copy(k, None).start()
             rest(c, False)
             for i in reversed(range(h)):
-                away_product(i, c, c == chunks - 1)
+                away_product(i, c)
+                if i == 0 and c == chunks - 1:
+                    pl.when(late)(functools.partial(away_send, i, c - 1))
+                if i > 0 or c != chunks - 2:
+                    away_send(i, c, c == chunks - 1)
+                else:
+                    pl.when(jnp.logical_not(late))(functools.partial(away_send, i, c))
             own_product(c)
 
     @pl.when(jnp.logical_not(is_inner))

time: 97.7 us -> 96.6 us (0.989)
  Pallas kernels: 96.9 us -> 95.4 us
    pallas_call x1, Pallas kernels: 95.7 us -> 94.2 us  [per_device(): pl.pallas_call(functools.partial(kernel, groups, replicas, width), out_sh...]
where the time goes in v6:
time: 96.6 us; the launch traced here: 96 us
  Pallas kernels  95.4 us (99%)
    pallas_call x1, Pallas kernels, per_device(): pl.pallas_call(functools.partial(kernel, groups, replicas, width), out_sh...  94.2 us

profile of v6, /device:TPU:0, one launch (start us, length us, event | category | flops | bytes accessed | tf_op | source)
XLA Modules:
  0.0 96.0 jit_solution(14399685387776032657)
XLA Ops:
  0.6 94.2 %shard_map.137 = (bf16[256,1024]{1,0:T(8,128)(2,1)S(1)}, bf16[256,1024]{1,0:T(8,128)(2,1)S(1)}, f32[32,1024]{1,0:T(8,128)S(1)}, f32[32,1024]{1,0:T(8,128)S(1)}, bf16[32,4096]{1,0:T(8,128)(2,1)S(1)}) custom-call(bf16[256,4096]{1,0:T(8,128)(2,1)} %bitcast.8, bf16[1,512]{1,0:T(2,128)(2,1)} %gain.1, bf16[512,1024]{1,0:T(8,128)(2,1)} %bitcast.9, ...), custom_call_target="tpu_custom_call" | custom-call | tf_op jit(solution)/shard_map/pallas_call | solution.py:498
  94.8 1.2 %shard_map.138 = (bf16[256,1024]{1,0:T(8,128)(2,1)}, bf16[256,1024]{1,0:T(8,128)(2,1)}, f32[32,1024]{1,0:T(8,128)}, f32[32,1024]{1,0:T(8,128)}, bf16[32,4096]{1,0:T(8,128)(2,1)}) custom-call(bf16[256,1024]{1,0:T(8,128)(2,1)S(1)} %get-tuple-element.15.refs_0_, bf16[256,1024]{1,0:T(8,128)(2,1)S(1)} %get-tuple-element.16.refs_1_, ...), custom_call_target="tpu_custom_call" | custom-call | tf_op jit(solution)/shard_map/pallas_call | solution.py:550

commit v7 on v6

--- a/solution.py
+++ b/solution.py
@@ -396,9 +396,9 @@
     @pl.when(jnp.logical_not(is_inner))
     def _():
         for c in range(chunks):
-            for j, (dist, _) in enumerate(outer_peers):
+            for j, (dist, inner) in enumerate(outer_peers):
                 from_peer(c, dist)
-                if c >= early:
+                if c >= early or not inner:
                     f_copy(c, j, dist).start()
             if early <= c < split:
                 x_copy(c, None).start()
@@ -459,16 +459,19 @@
     left(weights.at[:, rows(my_slot)], x_send)
     for j in range(h - 1):
         left(weights.at[:, rows(my_slot)], z_send.at[j])
-        left(weights.at[pl.ds(0, split), rows(my_slot)], f_send.at[j])
 
     @pl.when(is_inner)
     def _():
         for j in range(h - 1):
+            left(weights.at[pl.ds(0, split), rows(my_slot)], f_send.at[j])
             left(weights.at[pl.ds(0, early), rows(my_slot)], e_send.at[j])
 
     @pl.when(jnp.logical_not(is_inner))
     def _():
         left(weights.at[pl.ds(0, early), rows(my_slot)], e_send.at[0])
+        for j, (_, inner) in enumerate(outer_peers):
+            passed = split if inner else chunks
+            left(weights.at[pl.ds(0, passed), rows(my_slot)], f_send.at[j])
 
     landed(c_in.at[chunks - 1], c_recv.at[1])
     values[:, pl.ds((per_weight - 1) * width, width)] = summed(chunks - 1).astype(jnp.bfloat16)

time: 96.6 us -> 96.6 us (level)
  no operation moved by 1% of the time
where the time goes in v7:
time: 96.6 us; the launch traced here: 96 us
  Pallas kernels  95.4 us (99%)
    pallas_call x1, Pallas kernels, per_device(): pl.pallas_call(functools.partial(kernel, groups, replicas, width), out_sh...  94.2 us

profile of v7, /device:TPU:0, one launch (start us, length us, event | category | flops | bytes accessed | tf_op | source)
XLA Modules:
  0.0 96.0 jit_solution(17116920308453497431)
XLA Ops:
  0.6 94.2 %shard_map.137 = (bf16[256,1024]{1,0:T(8,128)(2,1)S(1)}, bf16[256,1024]{1,0:T(8,128)(2,1)S(1)}, f32[32,1024]{1,0:T(8,128)S(1)}, f32[32,1024]{1,0:T(8,128)S(1)}, bf16[32,4096]{1,0:T(8,128)(2,1)S(1)}) custom-call(bf16[256,4096]{1,0:T(8,128)(2,1)} %bitcast.8, bf16[1,512]{1,0:T(2,128)(2,1)} %gain.1, bf16[512,1024]{1,0:T(8,128)(2,1)} %bitcast.9, ...), custom_call_target="tpu_custom_call" | custom-call | tf_op jit(solution)/shard_map/pallas_call | solution.py:501
  94.8 1.2 %shard_map.138 = (bf16[256,1024]{1,0:T(8,128)(2,1)}, bf16[256,1024]{1,0:T(8,128)(2,1)}, f32[32,1024]{1,0:T(8,128)}, f32[32,1024]{1,0:T(8,128)}, bf16[32,4096]{1,0:T(8,128)(2,1)}) custom-call(bf16[256,1024]{1,0:T(8,128)(2,1)S(1)} %get-tuple-element.15.refs_0_, bf16[256,1024]{1,0:T(8,128)(2,1)S(1)} %get-tuple-element.16.refs_1_, ...), custom_call_target="tpu_custom_call" | custom-call | tf_op jit(solution)/shard_map/pallas_call | solution.py:553

commit v8 on v7

--- a/solution.py
+++ b/solution.py
@@ -385,12 +385,25 @@
             rest(c, False)
             for i in reversed(range(h)):
                 away_product(i, c)
-                if i == 0 and c == chunks - 1:
-                    pl.when(late)(functools.partial(away_send, i, c - 1))
-                if i > 0 or c != chunks - 2:
-                    away_send(i, c, c == chunks - 1)
-                else:
-                    pl.when(jnp.logical_not(late))(functools.partial(away_send, i, c))
+                if c < chunks - 2:
+                    away_send(i, c)
+
+            if c >= chunks - 2:
+                final = c == chunks - 1
+
+                @pl.when(late)
+                def _():
+                    for i in range(h - 1, 0, -1):
+                        away_send(i, c, final)
+                    if final:
+                        away_send(0, c - 1)
+                        away_send(0, c, True)
+
+                @pl.when(jnp.logical_not(late))
+                def _():
+                    for i in range(h):
+                        away_send(i, c, final)
+
             own_product(c)
 
     @pl.when(jnp.logical_not(is_inner))

time: 96.6 us -> 96.6 us (level)
  no operation moved by 1% of the time
where the time goes in v8:
time: 96.6 us; the launch traced here: 96 us
  Pallas kernels  95.4 us (99%)
    pallas_call x1, Pallas kernels, per_device(): pl.pallas_call(functools.partial(kernel, groups, replicas, width), out_sh...  94.2 us

profile of v8, /device:TPU:0, one launch (start us, length us, event | category | flops | bytes accessed | tf_op | source)
XLA Modules:
  0.0 96.0 jit_solution(1039610952649196146)
XLA Ops:
  0.6 94.2 %shard_map.137 = (bf16[256,1024]{1,0:T(8,128)(2,1)S(1)}, bf16[256,1024]{1,0:T(8,128)(2,1)S(1)}, f32[32,1024]{1,0:T(8,128)S(1)}, f32[32,1024]{1,0:T(8,128)S(1)}, bf16[32,4096]{1,0:T(8,128)(2,1)S(1)}) custom-call(bf16[256,4096]{1,0:T(8,128)(2,1)} %bitcast.8, bf16[1,512]{1,0:T(2,128)(2,1)} %gain.1, bf16[512,1024]{1,0:T(8,128)(2,1)} %bitcast.9, ...), custom_call_target="tpu_custom_call" | custom-call | tf_op jit(solution)/shard_map/pallas_call | solution.py:514
  94.8 1.2 %shard_map.138 = (bf16[256,1024]{1,0:T(8,128)(2,1)}, bf16[256,1024]{1,0:T(8,128)(2,1)}, f32[32,1024]{1,0:T(8,128)}, f32[32,1024]{1,0:T(8,128)}, bf16[32,4096]{1,0:T(8,128)(2,1)}) custom-call(bf16[256,1024]{1,0:T(8,128)(2,1)S(1)} %get-tuple-element.15.refs_0_, bf16[256,1024]{1,0:T(8,128)(2,1)S(1)} %get-tuple-element.16.refs_1_, ...), custom_call_target="tpu_custom_call" | custom-call | tf_op jit(solution)/shard_map/pallas_call | solution.py:566

commit v9 on v7

--- a/solution.py
+++ b/solution.py
@@ -89,13 +89,13 @@
     def greet(target):
         pl.semaphore_signal(barrier, inc=1, device_id=target, device_id_type=MESH)
 
+    pl.when(is_inner)(functools.partial(greet, other_half(0)))
     greet(partner)
     for j in range(1, replicas):
         greet({"replica": replica_at(j)})
 
     @pl.when(is_inner)
     def _():
-        greet(other_half(0))
         for dist, _ in inner_peers:
             greet(device(dist, x))
 
@@ -206,9 +206,9 @@
 
     @pl.when(is_inner)
     def _():
-        send_gain(inner_peers)
         hs_copy.wait()
         a_copy.start()
+        send_gain(inner_peers)
         lead_copy.wait()
         for c in range(chunks):
             if c == 1:

time: 96.6 us -> 96.6 us (level)
  no operation moved by 1% of the time
where the time goes in v9:
time: 96.6 us; the launch traced here: 96 us
  Pallas kernels  95.3 us (99%)
    pallas_call x1, Pallas kernels, per_device(): pl.pallas_call(functools.partial(kernel, groups, replicas, width), out_sh...  94.2 us

profile of v9, /device:TPU:0, one launch (start us, length us, event | category | flops | bytes accessed | tf_op | source)
XLA Modules:
  0.0 96.0 jit_solution(17731266643533889964)
XLA Ops:
  0.6 94.2 %shard_map.137 = (bf16[256,1024]{1,0:T(8,128)(2,1)S(1)}, bf16[256,1024]{1,0:T(8,128)(2,1)S(1)}, f32[32,1024]{1,0:T(8,128)S(1)}, f32[32,1024]{1,0:T(8,128)S(1)}, bf16[32,4096]{1,0:T(8,128)(2,1)S(1)}) custom-call(bf16[256,4096]{1,0:T(8,128)(2,1)} %bitcast.8, bf16[1,512]{1,0:T(2,128)(2,1)} %gain.1, bf16[512,1024]{1,0:T(8,128)(2,1)} %bitcast.9, ...), custom_call_target="tpu_custom_call" | custom-call | tf_op jit(solution)/shard_map/pallas_call | solution.py:501
  94.8 1.2 %shard_map.138 = (bf16[256,1024]{1,0:T(8,128)(2,1)}, bf16[256,1024]{1,0:T(8,128)(2,1)}, f32[32,1024]{1,0:T(8,128)}, f32[32,1024]{1,0:T(8,128)}, bf16[32,4096]{1,0:T(8,128)(2,1)}) custom-call(bf16[256,1024]{1,0:T(8,128)(2,1)S(1)} %get-tuple-element.15.refs_0_, bf16[256,1024]{1,0:T(8,128)(2,1)S(1)} %get-tuple-element.16.refs_1_, ...), custom_call_target="tpu_custom_call" | custom-call | tf_op jit(solution)/shard_map/pallas_call | solution.py:553
